TPU v7x, 128 devices: a whole 4x4x4 slice. The times are simulated.
128 devices in a mesh: batch: 1, outer: 2 (over core), rows: 64 (over z, y, x).
Axes of the slice: x: 4, y: 4, z: 4, core: 2. Of those that a mesh axis runs over, the one named last changes fastest.
Arguments:
- a_mat: float32 [131072, 1024], P(('batch', 'outer', 'rows'))
Outputs:
- output 1: float32 [131072, 1024], P(('batch', 'outer', 'rows'))
- output 2: float32 [1024, 1024], P('batch')
All inputs are finite; a program needn't handle non-finite values.
Results may differ from a plain program's by a relative error of at most 0.001.
Values sent between devices are 32-bit elements.
A program may use at most 1 GiB of HBM per device.

v0:
```python
import functools

import jax
import jax.numpy as jnp
from jax import lax
from jax.experimental import pallas as pl
from jax.experimental.pallas import tpu as pltpu
from jax.sharding import PartitionSpec as P

HI = lax.Precision.HIGHEST
N = 1024
NB = 128
SUB = 8


def mm(a, b):
    return lax.dot_general(a, b, (((1,), (0,)), ((), ())), precision=HI, preferred_element_type=jnp.float32)


def mm_tn(a, b):
    return lax.dot_general(a, b, (((0,), (0,)), ((), ())), precision=HI, preferred_element_type=jnp.float32)


def mm_nt(a, b):
    return lax.dot_general(a, b, (((1,), (1,)), ((), ())), precision=HI, preferred_element_type=jnp.float32)


def lane(v, c):
    return jnp.broadcast_to(v[:, c:c + 1], (SUB, NB))


PB = 256
NP = N // PB


def ds(i, n):
    return pl.ds(pl.multiple_of(i * n, n), n)


def loop(lo, hi, body):
    def step(i, carry):
        body(i)
        return carry
    lax.fori_loop(lo, hi, step, 0)


def factor_diag(s_ref, tasks=()):
    groups = NB // SUB
    tasks = list(tasks)
    for g in range(groups):
        base = SUB * g
        t = []
        for i in range(SUB):
            t.append([jnp.broadcast_to(s_ref[base + i:base + i + 1, h * NB:(h + 1) * NB], (SUB, NB)) for h in range(2)])
        a = {}
        for i in range(SUB):
            for j in range(i, SUB):
                a[i, j] = lane(t[i][0], base + j)
        inv = []
        u = {}
        rows = []
        for j in range(SUB):
            rs = lax.rsqrt(a[j, j])
            inv.append(rs)
            for i in range(j + 1, SUB):
                u[j, i] = a[j, i] * rs
            for i in range(j + 1, SUB):
                for i2 in range(i, SUB):
                    a[i, i2] = a[i, i2] - u[j, i] * u[j, i2]
            row = [t[j][h] * rs for h in range(2)]
            rows.append(row)
            for i in range(j + 1, SUB):
                for h in range(2):
                    t[i][h] = t[i][h] - u[j, i] * row[h]
        for j in range(SUB):
            for h in range(2):
                s_ref[base + j:base + j + 1, h * NB:(h + 1) * NB] = rows[j][h][0:1, :]
        for r in range(g + 1, groups):
            blk = [s_ref[SUB * r:SUB * r + SUB, h * NB:(h + 1) * NB] for h in range(2)]
            v = [lane(blk[0], base + j) for j in range(SUB)]
            for j in range(SUB):
                m = v[j] * inv[j]
                for j2 in range(j + 1, SUB):
                    v[j2] = v[j2] - m * u[j, j2]
                for h in range(2):
                    blk[h] = blk[h] - m * rows[j][h]
            for h in range(2):
                s_ref[SUB * r:SUB * r + SUB, h * NB:(h + 1) * NB] = blk[h]
        if g % 2 == 1 and tasks:
            tasks.pop(0)()
    for task in tasks:
        task()


def sweep_body(w_ref, q_ref, s_ref, inv_ref, prev_ref):
    r = lax.broadcasted_iota(jnp.int32, (NB, NB), 0)
    c = lax.broadcasted_iota(jnp.int32, (NB, NB), 1)

    def diag(k, h, tasks=()):
        rows = ds(k, NB)
        s_ref[:, :NB] = w_ref[rows, rows]
        s_ref[:, NB:] = jnp.where(r == c, 1.0, 0.0).astype(jnp.float32)
        factor_diag(s_ref, tasks)
        w_ref[rows, rows] = jnp.where(c >= r, s_ref[:, :NB], 0.0)
        inv_ref[ds(h, NB), ds(h, NB)] = s_ref[:, NB:]

    def after_first(p):
        top, nxt = ds(2 * p, NB), ds(2 * p + 1, NB)
        u01 = mm(inv_ref[:NB, :NB], w_ref[top, nxt])
        w_ref[top, nxt] = u01
        w_ref[nxt, nxt] = w_ref[nxt, nxt] - mm_tn(u01, u01)
        w_ref[nxt, top] = jnp.zeros((NB, NB), jnp.float32)

    def after_second(p):
        pr = ds(p, PB)
        i0 = inv_ref[:NB, :NB]
        i1 = inv_ref[NB:, NB:]
        inv_ref[NB:, :NB] = -mm(i1, mm_tn(w_ref[ds(2 * p, NB), ds(2 * p + 1, NB)], i0))
        inv_ref[:NB, NB:] = jnp.zeros((NB, NB), jnp.float32)
        prev_ref[...] = inv_ref[...]

        def panel_row(j):
            w_ref[pr, ds(j, PB)] = mm(inv_ref[...], w_ref[pr, ds(j, PB)])
            w_ref[ds(j, PB), pr] = jnp.zeros((PB, PB), jnp.float32)
        loop(p + 1, NP, panel_row)

        def trail(i):
            def cols(j):
                w_ref[ds(i, PB), ds(j, PB)] = w_ref[ds(i, PB), ds(j, PB)] - mm_tn(w_ref[pr, ds(i, PB)], w_ref[pr, ds(j, PB)])
            loop(i, NP, cols)
        loop(p + 1, NP, trail)

    def solve(m, q):
        q_ref[ds(m, PB), ds(q, PB)] = mm_nt(q_ref[ds(m, PB), ds(q, PB)], prev_ref[...])

    def update(m, s, d):
        q_ref[ds(m, PB), ds(d, PB)] = q_ref[ds(m, PB), ds(d, PB)] - mm(q_ref[ds(m, PB), ds(s, PB)], w_ref[ds(s, PB), ds(d, PB)])

    def first_panel(h):
        diag(h, h)
        @pl.when(h == 0)
        def _():
            after_first(0)
    loop(0, 2, first_panel)
    after_second(0)

    def panel(p):
        q = p - 1
        s3 = jnp.where(p == 3, 1, 0)
        d3 = jnp.where(p == 1, 2, 3)
        diag(2 * p, 0, [functools.partial(solve, m, q) for m in range(4)] + [functools.partial(update, m, s3, d3) for m in range(2)])
        after_first(p)
        diag(2 * p + 1, 1, [functools.partial(update, m, q, p) for m in range(4)] + [functools.partial(update, m, s3, d3) for m in range(2, 4)])
        after_second(p)
    loop(1, NP, panel)
    loop(0, NP, lambda m: solve(m, NP - 1))


VM = pl.BlockSpec(memory_space=pltpu.VMEM)
GRAM_VMEM = 18 * 1024 * 1024
SWEEP_VMEM = 30 * 1024 * 1024
MESH = pl.DeviceIdType.MESH
TILE = 8
BT = NB // TILE
NBLK = N // NB
HALF = NBLK * (NBLK + 1) // 4 * BT
COL = HALF // 3
QA = COL // 4
QB = QA // 4
AXES = ((0, 1, 2), (1, 2, 0), (2, 0, 1))
STRIDE = (1, 4, 16)
PANELS = (0, 3, 1, 2)


def block_slots():
    slots = {}
    for p in PANELS:
        for i in (2 * p, 2 * p + 1):
            for j in range(i, NBLK):
                slots[i, j] = len(slots)
    return slots


SLOT = block_slots()


def gram_reduce_kernel(a_ref, out_ref, snd, mine, rcv0, rcva, rcvb, rcvc, s_snd, s_rcv):
    core = lax.axis_index("outer")
    row = lax.axis_index("rows")
    pos = (lax.rem(row, 4), lax.rem(row // 4, 4), row // 16)
    partner = (0, 1 - core, row)

    def along(axis, d):
        there = lax.rem(pos[axis] + d, 4)
        return there, (0, core, row + (there - pos[axis]) * STRIDE[axis])

    barrier = pltpu.get_barrier_semaphore()
    peers = [partner] + [along(axis, d)[1] for axis in range(3) for d in (1, 2, 3)]
    for peer in peers:
        pl.semaphore_signal(barrier, inc=1, device_id=peer, device_id_type=MESH)

    count = [0]

    def copy(src, dst, peer):
        k = count[0]
        count[0] += 1
        return pltpu.make_async_remote_copy(src_ref=src, dst_ref=dst, send_sem=s_snd.at[k], recv_sem=s_rcv.at[k], device_id=peer, device_id_type=MESH)

    def products(dst, s):
        def block(t):
            part = (1 - s) * (t // 4) + s * (t // 3)
            p = (1 - s) * 3 * part + s * (1 + part)
            q = (1 - s) * (t - part) + s * (t + 1 - 2 * part)
            first = (15 - 4 * s) * part
            second = first + N // NB - 2 * p - 1
            g = mm_tn(a_ref[:, ds(p, PB)], a_ref[:, ds(q, PB)])
            for i, j in ((1, 0), (0, 0), (0, 1), (1, 1)):
                k = ((first, second)[i] + 2 * (q - p) + j) * BT
                dst[pl.ds(k, BT)] = g[i * NB:(i + 1) * NB, j * NB:(j + 1) * NB].reshape(BT, TILE, NB)
        loop(0, 5, block)

    products(snd, 1 - core)
    pl.semaphore_wait(barrier, len(peers))
    swap = copy(snd, rcv0, partner)
    swap.start()
    products(mine, core)
    swap.wait()
    mine[...] = mine[...] + rcv0[...]

    first = []
    for c in range(3):
        ax = AXES[c][0]
        for d in (1, 2, 3):
            there, peer = along(ax, d)
            cp = copy(mine.at[pl.ds(COL * c + QA * there, QA)], rcva.at[c, d - 1], peer)
            cp.start()
            first.append(cp)
    second = []
    for c in range(3):
        for cp in first[3 * c:3 * c + 3]:
            cp.wait_recv()
        off = COL * c + QA * pos[AXES[c][0]]
        mine[pl.ds(off, QA)] = (mine[pl.ds(off, QA)] + rcva[c, 0]) + (rcva[c, 1] + rcva[c, 2])
        for d in (1, 2, 3):
            there, peer = along(AXES[c][1], d)
            cp = copy(mine.at[pl.ds(off + QB * there, QB)], rcvb.at[c, d - 1], peer)
            cp.start()
            second.append(cp)
    third = []
    for c in range(3):
        for cp in second[3 * c:3 * c + 3]:
            cp.wait_recv()
        off = COL * c + QA * pos[AXES[c][0]] + QB * pos[AXES[c][1]]
        here = pos[AXES[c][2]]
        rcvc[c, here] = (mine[pl.ds(off, QB)] + rcvb[c, 0]) + (rcvb[c, 1] + rcvb[c, 2])
        for d in (1, 2, 3):
            _, peer = along(AXES[c][2], d)
            cp = copy(rcvc.at[c, here], rcvc.at[c, here], peer)
            cp.start()
            third.append(cp)
    fourth = []
    for c in range(3):
        for cp in third[3 * c:3 * c + 3]:
            cp.wait()
        off = core * HALF + COL * c + QA * pos[AXES[c][0]] + QB * pos[AXES[c][1]]
        out_ref[pl.ds(off, QB)] = ((rcvc[c, 0] + rcvc[c, 1]) + rcvc[c, 2]) + rcvc[c, 3]
        for d in (1, 2, 3):
            _, peer = along(AXES[c][1], d)
            cp = copy(out_ref.at[pl.ds(off, QB)], out_ref.at[pl.ds(off, QB)], peer)
            cp.start()
            fourth.append(cp)
    fifth = []
    last = []
    for c in range(3):
        for cp in fourth[3 * c:3 * c + 3]:
            cp.wait_recv()
        off = core * HALF + COL * c + QA * pos[AXES[c][0]]
        for d in (1, 2, 3):
            _, peer = along(AXES[c][0], d)
            cp = copy(out_ref.at[pl.ds(off, QA)], out_ref.at[pl.ds(off, QA)], peer)
            cp.start()
            fifth.append(cp)
        cp = copy(out_ref.at[pl.ds(off, QA)], out_ref.at[pl.ds(off, QA)], partner)
        cp.start()
        last.append(cp)
    for c in range(3):
        for d in (1, 2, 3):
            cp = fifth[3 * c + d - 1]
            cp.wait_recv()
            off = core * HALF + COL * c + QA * lax.rem(pos[AXES[c][0]] + 4 - d, 4)
            fw = copy(out_ref.at[pl.ds(off, QA)], out_ref.at[pl.ds(off, QA)], partner)
            fw.start()
            last.append(fw)
    for cp in first + second + fourth + fifth:
        cp.wait_send()
    for cp in last:
        cp.wait()
    assert count[0] == NCOPY


NCOPY = 1 + 9 * 5 + 12


def gram_reduce(a, collective_id=0):
    f32 = jnp.float32
    return pl.pallas_call(
        gram_reduce_kernel,
        out_shape=jax.ShapeDtypeStruct((2 * HALF, TILE, NB), f32),
        in_specs=[VM], out_specs=VM,
        scratch_shapes=[
            pltpu.VMEM((HALF, TILE, NB), f32), pltpu.VMEM((HALF, TILE, NB), f32), pltpu.VMEM((HALF, TILE, NB), f32),
            pltpu.VMEM((3, 3, QA, TILE, NB), f32), pltpu.VMEM((3, 3, QB, TILE, NB), f32), pltpu.VMEM((3, 4, QB, TILE, NB), f32),
            pltpu.SemaphoreType.DMA((NCOPY,)), pltpu.SemaphoreType.DMA((NCOPY,))],
        compiler_params=pltpu.CompilerParams(vmem_limit_bytes=GRAM_VMEM, collective_id=collective_id, has_side_effects=True))(a)


def unpack(g_ref, u_ref):
    for (i, j), s in SLOT.items():
        u_ref[i * NB:(i + 1) * NB, j * NB:(j + 1) * NB] = g_ref[s * BT:(s + 1) * BT].reshape(NB, NB)


def first_kernel(g_ref, b_ref, u_ref, q_ref, s_ref, inv_ref, prev_ref):
    unpack(g_ref, u_ref)
    q_ref[...] = b_ref[...]
    sweep_body(u_ref, q_ref, s_ref, inv_ref, prev_ref)


def second_kernel(g_ref, b_ref, u1_ref, r_ref, q_ref, u_ref, s_ref, inv_ref, prev_ref):
    unpack(g_ref, u_ref)
    q_ref[...] = b_ref[...]
    sweep_body(u_ref, q_ref, s_ref, inv_ref, prev_ref)
    r_ref[...] = jnp.zeros((N, N), jnp.float32)

    def ri(i):
        def rj(j):
            def rk(k):
                r_ref[ds(i, PB), ds(j, PB)] = r_ref[ds(i, PB), ds(j, PB)] + mm(u_ref[ds(i, PB), ds(k, PB)], u1_ref[ds(k, PB), ds(j, PB)])
            loop(i, j + 1, rk)
        loop(i, NP, rj)
    loop(0, NP, ri)


SQ = jax.ShapeDtypeStruct((N, N), jnp.float32)
WORK = [pltpu.VMEM((NB, 2 * NB), jnp.float32), pltpu.VMEM((PB, PB), jnp.float32), pltpu.VMEM((PB, PB), jnp.float32)]


def first_sweep(g, a):
    return pl.pallas_call(first_kernel, out_shape=[SQ, SQ], in_specs=[VM] * 2, out_specs=[VM] * 2, scratch_shapes=WORK, compiler_params=pltpu.CompilerParams(vmem_limit_bytes=SWEEP_VMEM))(g, a)


def second_sweep(g, q, u1):
    return pl.pallas_call(second_kernel, out_shape=[SQ, SQ], in_specs=[VM] * 3, out_specs=[VM] * 2, scratch_shapes=[pltpu.VMEM((N, N), jnp.float32)] + WORK, compiler_params=pltpu.CompilerParams(vmem_limit_bytes=SWEEP_VMEM))(g, q, u1)


def solution(mesh):
    row_spec = P(("batch", "outer", "rows"), None)

    def group_qr(a_block):
        u1, q1 = first_sweep(gram_reduce(a_block, 0), a_block)
        r_block, q_block = second_sweep(gram_reduce(q1, 1), q1, u1)
        return q_block, r_block

    return jax.shard_map(group_qr, mesh=mesh, in_specs=(row_spec,), out_specs=(row_spec, P("batch", None)), check_vma=False)
```

profile of v0, /device:TPU:1, one launch (start us, length us, event | category | flops | bytes accessed | tf_op | source)
XLA Modules:
  0.0 186.8 jit_solution(8896282132491950609)
XLA Ops:
  0.6 0.0 copy-start
  0.6 2.2 %copy-done = f32[1024,1024]{1,0:T(8,128)S(1)} copy-done((f32[1024,1024]{1,0:T(8,128)S(1)}, f32[1024,1024]{1,0:T(8,128)}, u32[]{:S(2)}) %copy-start) | copy-done | bytes 4194328
  2.8 0.0 copy-start.1
  2.8 46.1 %shard_map.30.g_ref = f32[576,8,128]{2,1,0:T(8,128)S(1)} custom-call(f32[1024,1024]{1,0:T(8,128)S(1)} %copy-done), custom_call_target="tpu_custom_call" | custom-call | tf_op jit(solution)/shard_map/pallas_call | solution.py:306
  48.9 0.0 copy-done.1
  49.0 43.1 %shard_map.31 = (f32[1024,1024]{1,0:T(8,128)S(1)}, f32[1024,1024]{1,0:T(8,128)S(1)}) custom-call(f32[576,8,128]{2,1,0:T(8,128)S(1)} %shard_map.30.g_ref, f32[1024,1024]{1,0:T(8,128)S(1)} %copy-done.1), custom_call_target="tpu_custom_call" | custom-call | tf_op jit(solution)/shard_map/pallas_call | solution.py:348
  92.0 40.6 %shard_map.32.g_ref = f32[576,8,128]{2,1,0:T(8,128)S(1)} custom-call(f32[1024,1024]{1,0:T(8,128)S(1)} %get-tuple-element.6.a_ref.b_ref), custom_call_target="tpu_custom_call" | custom-call | tf_op jit(solution)/shard_map/pallas_call | solution.py:306
  132.6 54.2 %shard_map.33 = (f32[1024,1024]{1,0:T(8,128)}, f32[1024,1024]{1,0:T(8,128)}) custom-call(f32[576,8,128]{2,1,0:T(8,128)S(1)} %shard_map.32.g_ref, f32[1024,1024]{1,0:T(8,128)S(1)} %get-tuple-element.6.a_ref.b_ref, f32[1024,1024]{1,0:T(8,128)S(1)} %get-tuple-element.7.u1_ref), custom_call_target="tpu_custom_call" | custom-call | tf_op jit(solution)/shard_map/pallas_call | solution.py:352
Async XLA Ops:
  0.6 2.2 %copy-start = (f32[1024,1024]{1,0:T(8,128)S(1)}, f32[1024,1024]{1,0:T(8,128)}, u32[]{:S(2)}) copy-start(f32[1024,1024]{1,0:T(8,128)} %b_ref.1) | copy-start | bytes 12582916
  2.8 46.1 %copy-start.1 = (f32[1024,1024]{1,0:T(8,128)S(1)}, f32[1024,1024]{1,0:T(8,128)}, u32[]{:S(2)}) copy-start(f32[1024,1024]{1,0:T(8,128)} %b_ref.1) | copy-start | bytes 12582916
where the time goes:
time: 187 us
  Pallas kernels  184 us (98%)
  local copies, waits for them, and re-layouts  2.18 us (1%)
    pallas_call x2, Pallas kernels, gram_reduce(): pl.pallas_call(gram_reduce_kernel, out_shape=jax.ShapeDtypeStruct((2 * HA...  86.7 us
    pallas_call x1, Pallas kernels, second_sweep(): pl.pallas_call(second_kernel, out_shape=[SQ, SQ], in_specs=[VM] * 3, out_...  54.2 us
    pallas_call x1, Pallas kernels, first_sweep(): pl.pallas_call(first_kernel, out_shape=[SQ, SQ], in_specs=[VM] * 2, out_s...  43.1 us

commit v1 on v0

--- a/solution.py
+++ b/solution.py
@@ -44,48 +44,47 @@
     lax.fori_loop(lo, hi, step, 0)
 
 
+RG = 15
+
+
 def factor_diag(s_ref, tasks=()):
     groups = NB // SUB
     tasks = list(tasks)
     for g in range(groups):
         base = SUB * g
-        t = []
-        for i in range(SUB):
-            t.append([jnp.broadcast_to(s_ref[base + i:base + i + 1, h * NB:(h + 1) * NB], (SUB, NB)) for h in range(2)])
-        a = {}
-        for i in range(SUB):
-            for j in range(i, SUB):
-                a[i, j] = lane(t[i][0], base + j)
-        inv = []
-        u = {}
-        rows = []
+        left = jnp.stack([jnp.broadcast_to(s_ref[base + i:base + i + 1, :NB], (SUB, NB)) for i in range(SUB)])
+        right = jnp.stack([jnp.broadcast_to(s_ref[base + i:base + i + 1, NB:], (SUB, NB)) for i in range(SUB)])
+        a = [jnp.stack([lane(left[j], base + i) for i in range(j, SUB)]) for j in range(SUB)]
+        inv, u, rows = [], [], []
         for j in range(SUB):
-            rs = lax.rsqrt(a[j, j])
+            rs = lax.rsqrt(a[j][0])
             inv.append(rs)
-            for i in range(j + 1, SUB):
-                u[j, i] = a[j, i] * rs
-            for i in range(j + 1, SUB):
-                for i2 in range(i, SUB):
-                    a[i, i2] = a[i, i2] - u[j, i] * u[j, i2]
-            row = [t[j][h] * rs for h in range(2)]
-            rows.append(row)
-            for i in range(j + 1, SUB):
-                for h in range(2):
-                    t[i][h] = t[i][h] - u[j, i] * row[h]
-        for j in range(SUB):
-            for h in range(2):
-                s_ref[base + j:base + j + 1, h * NB:(h + 1) * NB] = rows[j][h][0:1, :]
-        for r in range(g + 1, groups):
-            blk = [s_ref[SUB * r:SUB * r + SUB, h * NB:(h + 1) * NB] for h in range(2)]
-            v = [lane(blk[0], base + j) for j in range(SUB)]
+            rl, rr = left[0] * rs, right[0] * rs
+            rows.append((rl, rr))
+            s_ref[base + j:base + j + 1, :NB] = rl[0:1]
+            s_ref[base + j:base + j + 1, NB:] = rr[0:1]
+            if j + 1 < SUB:
+                uj = a[j][1:] * rs
+                u.append(uj)
+                for i in range(j + 1, SUB):
+                    a[i] = a[i] - uj[i - j - 1:] * uj[i - j - 1]
+                left = left[1:] - uj * rl
+                right = right[1:] - uj * rr
+        for lo in range(g + 1, groups, RG):
+            hi = min(lo + RG, groups)
+            n = hi - lo
+            at = slice(SUB * lo, SUB * hi)
+            bl = s_ref[at, :NB].reshape(n, SUB, NB)
+            br = s_ref[at, NB:].reshape(n, SUB, NB)
+            v = [jnp.broadcast_to(bl[:, :, base + j:base + j + 1], (n, SUB, NB)) for j in range(SUB)]
             for j in range(SUB):
                 m = v[j] * inv[j]
                 for j2 in range(j + 1, SUB):
-                    v[j2] = v[j2] - m * u[j, j2]
-                for h in range(2):
-                    blk[h] = blk[h] - m * rows[j][h]
-            for h in range(2):
-                s_ref[SUB * r:SUB * r + SUB, h * NB:(h + 1) * NB] = blk[h]
+                    v[j2] = v[j2] - m * u[j][j2 - j - 1]
+                bl = bl - m * rows[j][0]
+                br = br - m * rows[j][1]
+            s_ref[at, :NB] = bl.reshape(n * SUB, NB)
+            s_ref[at, NB:] = br.reshape(n * SUB, NB)
         if g % 2 == 1 and tasks:
             tasks.pop(0)()
     for task in tasks:
@@ -301,16 +300,21 @@
 NCOPY = 1 + 9 * 5 + 12
 
 
+def comm_scratch():
+    f32 = jnp.float32
+    return [
+            pltpu.VMEM((HALF, TILE, NB), f32), pltpu.VMEM((HALF, TILE, NB), f32), pltpu.VMEM((HALF, TILE, NB), f32),
+            pltpu.VMEM((3, 3, QA, TILE, NB), f32), pltpu.VMEM((3, 3, QB, TILE, NB), f32), pltpu.VMEM((3, 4, QB, TILE, NB), f32),
+            pltpu.SemaphoreType.DMA((NCOPY,)), pltpu.SemaphoreType.DMA((NCOPY,))]
+
+
 def gram_reduce(a, collective_id=0):
     f32 = jnp.float32
     return pl.pallas_call(
         gram_reduce_kernel,
         out_shape=jax.ShapeDtypeStruct((2 * HALF, TILE, NB), f32),
         in_specs=[VM], out_specs=VM,
-        scratch_shapes=[
-            pltpu.VMEM((HALF, TILE, NB), f32), pltpu.VMEM((HALF, TILE, NB), f32), pltpu.VMEM((HALF, TILE, NB), f32),
-            pltpu.VMEM((3, 3, QA, TILE, NB), f32), pltpu.VMEM((3, 3, QB, TILE, NB), f32), pltpu.VMEM((3, 4, QB, TILE, NB), f32),
-            pltpu.SemaphoreType.DMA((NCOPY,)), pltpu.SemaphoreType.DMA((NCOPY,))],
+        scratch_shapes=comm_scratch(),
         compiler_params=pltpu.CompilerParams(vmem_limit_bytes=GRAM_VMEM, collective_id=collective_id, has_side_effects=True))(a)
 
 
@@ -319,10 +323,71 @@
         u_ref[i * NB:(i + 1) * NB, j * NB:(j + 1) * NB] = g_ref[s * BT:(s + 1) * BT].reshape(NB, NB)
 
 
-def first_kernel(g_ref, b_ref, u_ref, q_ref, s_ref, inv_ref, prev_ref):
+def tri_iota():
+    r = lax.broadcasted_iota(jnp.int32, (NB, NB), 0)
+    c = lax.broadcasted_iota(jnp.int32, (NB, NB), 1)
+    return r, c
+
+
+def sweep_one(w_ref, q_ref, s_ref, inv_ref):
+    r, c = tri_iota()
+
+    def panel(p):
+        def half(h):
+            k = 2 * p + h
+            rows = ds(k, NB)
+            s_ref[:, :NB] = w_ref[rows, rows]
+            s_ref[:, NB:] = jnp.where(r == c, 1.0, 0.0).astype(jnp.float32)
+            factor_diag(s_ref)
+            w_ref[rows, rows] = jnp.where(c >= r, s_ref[:, :NB], 0.0)
+            li = s_ref[:, NB:]
+            inv_ref[pl.ds(pl.multiple_of(h * NB, NB), NB), pl.ds(pl.multiple_of(h * NB, NB), NB)] = li
+            loop(k + 1, N // NB, lambda j: w_ref.__setitem__((rows, ds(j, NB)), mm(li, w_ref[rows, ds(j, NB)])))
+
+            @pl.when(h == 0)
+            def _():
+                nxt = ds(k + 1, NB)
+                lhs = w_ref[rows, nxt]
+                def upd(j):
+                    w_ref[nxt, ds(j, NB)] = w_ref[nxt, ds(j, NB)] - mm_tn(lhs, w_ref[rows, ds(j, NB)])
+                loop(k + 1, N // NB, upd)
+
+        loop(0, 2, half)
+        pr = ds(p, PB)
+        i0 = inv_ref[:NB, :NB]
+        i1 = inv_ref[NB:, NB:]
+        u01 = w_ref[ds(2 * p, NB), ds(2 * p + 1, NB)]
+        inv_ref[NB:, :NB] = -mm(i1, mm_tn(u01, i0))
+        inv_ref[:NB, NB:] = jnp.zeros((NB, NB), jnp.float32)
+
+        def trail(i):
+            def cols(j):
+                w_ref[ds(i, PB), ds(j, PB)] = w_ref[ds(i, PB), ds(j, PB)] - mm_tn(w_ref[pr, ds(i, PB)], w_ref[pr, ds(j, PB)])
+            loop(i, NP, cols)
+        loop(p + 1, NP, trail)
+
+        def chunk(m):
+            rr = ds(m, PB)
+            def prev(t):
+                q_ref[rr, pr] = q_ref[rr, pr] - mm(q_ref[rr, ds(t, PB)], w_ref[ds(t, PB), pr])
+            loop(0, p, prev)
+            q_ref[rr, pr] = mm_nt(q_ref[rr, pr], inv_ref[...])
+        loop(0, N // PB, chunk)
+
+    loop(0, NP, panel)
+
+    def zero(k):
+        def zz(j):
+            w_ref[ds(k, NB), ds(j, NB)] = jnp.zeros((NB, NB), jnp.float32)
+        loop(0, k, zz)
+    loop(1, N // NB, zero)
+
+
+def fused_kernel(g_ref, b_ref, u_ref, q_ref, out_ref, s_ref, inv_ref, prev_ref, *rest):
     unpack(g_ref, u_ref)
     q_ref[...] = b_ref[...]
-    sweep_body(u_ref, q_ref, s_ref, inv_ref, prev_ref)
+    sweep_one(u_ref, q_ref, s_ref, inv_ref)
+    gram_reduce_kernel(q_ref, out_ref, *rest)
 
 
 def second_kernel(g_ref, b_ref, u1_ref, r_ref, q_ref, u_ref, s_ref, inv_ref, prev_ref):
@@ -345,7 +410,9 @@
 
 
 def first_sweep(g, a):
-    return pl.pallas_call(first_kernel, out_shape=[SQ, SQ], in_specs=[VM] * 2, out_specs=[VM] * 2, scratch_shapes=WORK, compiler_params=pltpu.CompilerParams(vmem_limit_bytes=SWEEP_VMEM))(g, a)
+    return pl.pallas_call(
+        fused_kernel, out_shape=[SQ, SQ, jax.ShapeDtypeStruct((2 * HALF, TILE, NB), jnp.float32)], in_specs=[VM] * 2, out_specs=[VM] * 3, scratch_shapes=WORK + comm_scratch(),
+        compiler_params=pltpu.CompilerParams(vmem_limit_bytes=SWEEP_VMEM, collective_id=1, has_side_effects=True))(g, a)
 
 
 def second_sweep(g, q, u1):
@@ -356,8 +423,8 @@
     row_spec = P(("batch", "outer", "rows"), None)
 
     def group_qr(a_block):
-        u1, q1 = first_sweep(gram_reduce(a_block, 0), a_block)
-        r_block, q_block = second_sweep(gram_reduce(q1, 1), q1, u1)
+        u1, q1, g2 = first_sweep(gram_reduce(a_block, 0), a_block)
+        r_block, q_block = second_sweep(g2, q1, u1)
         return q_block, r_block
 
     return jax.shard_map(group_qr, mesh=mesh, in_specs=(row_spec,), out_specs=(row_spec, P("batch", None)), check_vma=False)

time: 187 us -> 208 us (1.11)
  Pallas kernels: 184 us -> 205 us
    pallas_call x1, Pallas kernels: 43.1 us -> 103 us  [first_sweep(): pl.pallas_call(fused_kernel, out_shape=[SQ, SQ, jax.ShapeDtypeStruct((2 *...]
    pallas_call x2 -> x1, Pallas kernels: 86.7 us -> 46.1 us  [gram_reduce(): pl.pallas_call(gram_reduce_kernel, out_shape=jax.ShapeDtypeStruct((2 * HA...]
    pallas_call x1, Pallas kernels: 54.2 us -> 56.4 us  [second_sweep(): pl.pallas_call(second_kernel, out_shape=[SQ, SQ], in_specs=[VM] * 3, out_...]
where the time goes in v1:
time: 208 us
  Pallas kernels  205 us (99%)
  local copies, waits for them, and re-layouts  2.18 us (1%)
    pallas_call x1, Pallas kernels, first_sweep(): pl.pallas_call(fused_kernel, out_shape=[SQ, SQ, jax.ShapeDtypeStruct((2 *...  103 us
    pallas_call x1, Pallas kernels, second_sweep(): pl.pallas_call(second_kernel, out_shape=[SQ, SQ], in_specs=[VM] * 3, out_...  56.4 us
    pallas_call x1, Pallas kernels, gram_reduce(): pl.pallas_call(gram_reduce_kernel, out_shape=jax.ShapeDtypeStruct((2 * HA...  46.1 us

profile of v1, /device:TPU:1, one launch (start us, length us, event | category | flops | bytes accessed | tf_op | source)
XLA Modules:
  0.0 208.0 jit_solution(8527743126385918467)
XLA Ops:
  0.6 0.0 copy-start
  0.6 2.2 %copy-done = f32[1024,1024]{1,0:T(8,128)S(1)} copy-done((f32[1024,1024]{1,0:T(8,128)S(1)}, f32[1024,1024]{1,0:T(8,128)}, u32[]{:S(2)}) %copy-start) | copy-done | bytes 4194328
  2.8 0.0 copy-start.1
  2.8 46.1 %shard_map.30.g_ref = f32[576,8,128]{2,1,0:T(8,128)S(1)} custom-call(f32[1024,1024]{1,0:T(8,128)S(1)} %copy-done), custom_call_target="tpu_custom_call" | custom-call | tf_op jit(solution)/shard_map/pallas_call | solution.py:313
  48.9 0.0 copy-done.1
  49.0 102.7 %shard_map.31 = (f32[1024,1024]{1,0:T(8,128)S(1)}, f32[1024,1024]{1,0:T(8,128)S(1)}, f32[576,8,128]{2,1,0:T(8,128)S(1)}) custom-call(f32[576,8,128]{2,1,0:T(8,128)S(1)} %shard_map.30.g_ref, f32[1024,1024]{1,0:T(8,128)S(1)} %copy-done.1), custom_call_target="tpu_custom_call" | custom-call | tf_op jit(solution)/shard_map/pallas_call | solution.py:413
  151.7 56.4 %shard_map.32 = (f32[1024,1024]{1,0:T(8,128)}, f32[1024,1024]{1,0:T(8,128)}) custom-call(f32[576,8,128]{2,1,0:T(8,128)S(1)} %get-tuple-element.7.g_ref, f32[1024,1024]{1,0:T(8,128)S(1)} %get-tuple-element.8.b_ref, f32[1024,1024]{1,0:T(8,128)S(1)} %get-tuple-element.9.u1_ref), custom_call_target="tpu_custom_call" | custom-call | tf_op jit(solution)/shard_map/pallas_call | solution.py:419
Async XLA Ops:
  0.6 2.2 %copy-start = (f32[1024,1024]{1,0:T(8,128)S(1)}, f32[1024,1024]{1,0:T(8,128)}, u32[]{:S(2)}) copy-start(f32[1024,1024]{1,0:T(8,128)} %b_ref.1) | copy-start | bytes 12582916
  2.8 46.1 %copy-start.1 = (f32[1024,1024]{1,0:T(8,128)S(1)}, f32[1024,1024]{1,0:T(8,128)}, u32[]{:S(2)}) copy-start(f32[1024,1024]{1,0:T(8,128)} %b_ref.1) | copy-start | bytes 12582916

commit v2 on v1

--- a/solution.py
+++ b/solution.py
@@ -44,7 +44,7 @@
     lax.fori_loop(lo, hi, step, 0)
 
 
-RG = 15
+RG = 3
 
 
 def factor_diag(s_ref, tasks=()):
@@ -91,73 +91,10 @@
         task()
 
 
-def sweep_body(w_ref, q_ref, s_ref, inv_ref, prev_ref):
-    r = lax.broadcasted_iota(jnp.int32, (NB, NB), 0)
-    c = lax.broadcasted_iota(jnp.int32, (NB, NB), 1)
-
-    def diag(k, h, tasks=()):
-        rows = ds(k, NB)
-        s_ref[:, :NB] = w_ref[rows, rows]
-        s_ref[:, NB:] = jnp.where(r == c, 1.0, 0.0).astype(jnp.float32)
-        factor_diag(s_ref, tasks)
-        w_ref[rows, rows] = jnp.where(c >= r, s_ref[:, :NB], 0.0)
-        inv_ref[ds(h, NB), ds(h, NB)] = s_ref[:, NB:]
-
-    def after_first(p):
-        top, nxt = ds(2 * p, NB), ds(2 * p + 1, NB)
-        u01 = mm(inv_ref[:NB, :NB], w_ref[top, nxt])
-        w_ref[top, nxt] = u01
-        w_ref[nxt, nxt] = w_ref[nxt, nxt] - mm_tn(u01, u01)
-        w_ref[nxt, top] = jnp.zeros((NB, NB), jnp.float32)
-
-    def after_second(p):
-        pr = ds(p, PB)
-        i0 = inv_ref[:NB, :NB]
-        i1 = inv_ref[NB:, NB:]
-        inv_ref[NB:, :NB] = -mm(i1, mm_tn(w_ref[ds(2 * p, NB), ds(2 * p + 1, NB)], i0))
-        inv_ref[:NB, NB:] = jnp.zeros((NB, NB), jnp.float32)
-        prev_ref[...] = inv_ref[...]
-
-        def panel_row(j):
-            w_ref[pr, ds(j, PB)] = mm(inv_ref[...], w_ref[pr, ds(j, PB)])
-            w_ref[ds(j, PB), pr] = jnp.zeros((PB, PB), jnp.float32)
-        loop(p + 1, NP, panel_row)
-
-        def trail(i):
-            def cols(j):
-                w_ref[ds(i, PB), ds(j, PB)] = w_ref[ds(i, PB), ds(j, PB)] - mm_tn(w_ref[pr, ds(i, PB)], w_ref[pr, ds(j, PB)])
-            loop(i, NP, cols)
-        loop(p + 1, NP, trail)
-
-    def solve(m, q):
-        q_ref[ds(m, PB), ds(q, PB)] = mm_nt(q_ref[ds(m, PB), ds(q, PB)], prev_ref[...])
-
-    def update(m, s, d):
-        q_ref[ds(m, PB), ds(d, PB)] = q_ref[ds(m, PB), ds(d, PB)] - mm(q_ref[ds(m, PB), ds(s, PB)], w_ref[ds(s, PB), ds(d, PB)])
-
-    def first_panel(h):
-        diag(h, h)
-        @pl.when(h == 0)
-        def _():
-            after_first(0)
-    loop(0, 2, first_panel)
-    after_second(0)
-
-    def panel(p):
-        q = p - 1
-        s3 = jnp.where(p == 3, 1, 0)
-        d3 = jnp.where(p == 1, 2, 3)
-        diag(2 * p, 0, [functools.partial(solve, m, q) for m in range(4)] + [functools.partial(update, m, s3, d3) for m in range(2)])
-        after_first(p)
-        diag(2 * p + 1, 1, [functools.partial(update, m, q, p) for m in range(4)] + [functools.partial(update, m, s3, d3) for m in range(2, 4)])
-        after_second(p)
-    loop(1, NP, panel)
-    loop(0, NP, lambda m: solve(m, NP - 1))
-
-
 VM = pl.BlockSpec(memory_space=pltpu.VMEM)
 GRAM_VMEM = 18 * 1024 * 1024
-SWEEP_VMEM = 30 * 1024 * 1024
+SWEEP_VMEM = 42 * 1024 * 1024
+FINISH_VMEM = 24 * 1024 * 1024
 MESH = pl.DeviceIdType.MESH
 TILE = 8
 BT = NB // TILE
@@ -300,21 +237,16 @@
 NCOPY = 1 + 9 * 5 + 12
 
 
-def comm_scratch():
-    f32 = jnp.float32
-    return [
-            pltpu.VMEM((HALF, TILE, NB), f32), pltpu.VMEM((HALF, TILE, NB), f32), pltpu.VMEM((HALF, TILE, NB), f32),
-            pltpu.VMEM((3, 3, QA, TILE, NB), f32), pltpu.VMEM((3, 3, QB, TILE, NB), f32), pltpu.VMEM((3, 4, QB, TILE, NB), f32),
-            pltpu.SemaphoreType.DMA((NCOPY,)), pltpu.SemaphoreType.DMA((NCOPY,))]
-
-
 def gram_reduce(a, collective_id=0):
     f32 = jnp.float32
     return pl.pallas_call(
         gram_reduce_kernel,
         out_shape=jax.ShapeDtypeStruct((2 * HALF, TILE, NB), f32),
         in_specs=[VM], out_specs=VM,
-        scratch_shapes=comm_scratch(),
+        scratch_shapes=[
+            pltpu.VMEM((HALF, TILE, NB), f32), pltpu.VMEM((HALF, TILE, NB), f32), pltpu.VMEM((HALF, TILE, NB), f32),
+            pltpu.VMEM((3, 3, QA, TILE, NB), f32), pltpu.VMEM((3, 3, QB, TILE, NB), f32), pltpu.VMEM((3, 4, QB, TILE, NB), f32),
+            pltpu.SemaphoreType.DMA((NCOPY,)), pltpu.SemaphoreType.DMA((NCOPY,))],
         compiler_params=pltpu.CompilerParams(vmem_limit_bytes=GRAM_VMEM, collective_id=collective_id, has_side_effects=True))(a)
 
 
@@ -323,108 +255,281 @@
         u_ref[i * NB:(i + 1) * NB, j * NB:(j + 1) * NB] = g_ref[s * BT:(s + 1) * BT].reshape(NB, NB)
 
 
-def tri_iota():
+SIZES = (96, 192, 192, 288)
+COPIES = 1 + 9 * 5 + 12
+
+
+class PanelSum:
+    def __init__(self, n, buf, rcv0, rcva, rcvb, rcvc, out, s_snd, s_rcv, place):
+        self.size = SIZES[n]
+        self.half = self.size // 2
+        self.qa = self.half // 12
+        self.qb = self.qa // 4
+        self.buf, self.rcv0, self.rcva, self.rcvb, self.rcvc, self.out = buf, rcv0, rcva, rcvb, rcvc, out
+        self.s_snd, self.s_rcv = s_snd, s_rcv
+        self.core, self.pos, self.partner, self.along = place
+        self.own = self.core * self.half
+
+    def copy(self, k, src, dst, peer):
+        return pltpu.make_async_remote_copy(src_ref=src, dst_ref=dst, send_sem=self.s_snd.at[k], recv_sem=self.s_rcv.at[k], device_id=peer, device_id_type=MESH)
+
+    def offset(self, c, depth):
+        off = self.own + c * (self.half // 3)
+        if depth >= 1:
+            off = off + self.qa * self.pos[AXES[c][0]]
+        if depth >= 2:
+            off = off + self.qb * self.pos[AXES[c][1]]
+        return off
+
+    def copies(self, stage):
+        out = []
+        for d in (1, 3, 2):
+            for c in range(3):
+                k = 1 + 9 * stage + 3 * (d - 1) + c
+                axis = AXES[c][(0, 1, 2, 1, 0)[stage]]
+                there, peer = self.along(axis, d)
+                if stage == 0:
+                    src, dst = self.buf.at[pl.ds(self.offset(c, 0) + self.qa * there, self.qa)], self.rcva.at[c, d - 1]
+                elif stage == 1:
+                    src, dst = self.buf.at[pl.ds(self.offset(c, 1) + self.qb * there, self.qb)], self.rcvb.at[c, d - 1]
+                elif stage == 2:
+                    src = dst = self.rcvc.at[c, self.pos[axis]]
+                elif stage == 3:
+                    src = dst = self.out.at[pl.ds(self.offset(c, 2), self.qb)]
+                else:
+                    src = dst = self.out.at[pl.ds(self.offset(c, 1), self.qa)]
+                out.append(self.copy(k, src, dst, peer))
+        return out
+
+    def forwards(self):
+        out = []
+        for c in range(3):
+            for d in range(4):
+                off = self.offset(c, 0) + self.qa * lax.rem(self.pos[AXES[c][0]] + 4 - d, 4)
+                ref = self.out.at[pl.ds(off, self.qa)]
+                out.append(self.copy(46 + 4 * c + d, ref, ref, self.partner))
+        return out
+
+    def swap(self):
+        other = pl.ds(self.half - self.own, self.half)
+        return self.copy(0, self.buf.at[other], self.rcv0, self.partner)
+
+    def run(self, stage):
+        if stage == 0:
+            self.swap().start()
+            return
+        if stage == 1:
+            self.swap().wait()
+            at = pl.ds(self.own, self.half)
+            self.buf[at] = self.buf[at] + self.rcv0[...]
+        elif stage <= 6:
+            for cp in self.copies(stage - 2):
+                cp.wait()
+        if stage == 2:
+            for c in range(3):
+                at = pl.ds(self.offset(c, 1), self.qa)
+                self.buf[at] = (self.buf[at] + self.rcva[c, 0]) + (self.rcva[c, 1] + self.rcva[c, 2])
+        elif stage == 3:
+            for c in range(3):
+                self.rcvc[c, self.pos[AXES[c][2]]] = (self.buf[pl.ds(self.offset(c, 2), self.qb)] + self.rcvb[c, 0]) + (self.rcvb[c, 1] + self.rcvb[c, 2])
+        elif stage == 4:
+            for c in range(3):
+                self.out[pl.ds(self.offset(c, 2), self.qb)] = ((self.rcvc[c, 0] + self.rcvc[c, 1]) + self.rcvc[c, 2]) + self.rcvc[c, 3]
+        if stage <= 5:
+            for cp in self.copies(stage - 1):
+                cp.start()
+        elif stage == 6:
+            for cp in self.forwards():
+                cp.start()
+        else:
+            for cp in self.forwards():
+                cp.wait()
+
+
+POINTS = (
+    (2, ((0, 0),)), (3, ((1, 0),)), (4, ((2, 0), (0, 1))), (5, ((3, 0), (1, 1))), (6, ((4, 0), (2, 1), (0, 2))),
+    (7, ((5, 0), (3, 1), (1, 2))), (7.3, ((6, 0), (4, 1), (2, 2))), (7.6, ((0, 3), (7, 0), (5, 1), (3, 2))),
+    (8, ((1, 3), (6, 1), (4, 2))), (9, ((2, 3), (7, 1), (5, 2))), (10, ((3, 3), (6, 2))), (11, ((4, 3), (7, 2))),
+    (12, ((5, 3),)), (13, ((6, 3), (7, 3))))
+
+
+def sweeps_kernel(g_ref, a_ref, q_ref, w_ref, inv_ref, s_ref, rhs_ref, *rest):
+    core = lax.axis_index("outer")
+    row = lax.axis_index("rows")
+    pos = (lax.rem(row, 4), lax.rem(row // 4, 4), row // 16)
+    partner = (0, 1 - core, row)
+
+    def along(axis, d):
+        there = lax.rem(pos[axis] + d, 4)
+        return there, (0, core, row + (there - pos[axis]) * STRIDE[axis])
+
+    barrier = pltpu.get_barrier_semaphore()
+    peers = [partner] + [along(axis, d)[1] for axis in range(3) for d in (1, 2, 3)]
+    for peer in peers:
+        pl.semaphore_signal(barrier, inc=1, device_id=peer, device_id_type=MESH)
+
+    sums = [PanelSum(n, *rest[8 * n:8 * n + 8], (core, pos, partner, along)) for n in range(NP)]
     r = lax.broadcasted_iota(jnp.int32, (NB, NB), 0)
     c = lax.broadcasted_iota(jnp.int32, (NB, NB), 1)
-    return r, c
-
-
-def sweep_one(w_ref, q_ref, s_ref, inv_ref):
-    r, c = tri_iota()
-
-    def panel(p):
-        def half(h):
-            k = 2 * p + h
-            rows = ds(k, NB)
-            s_ref[:, :NB] = w_ref[rows, rows]
-            s_ref[:, NB:] = jnp.where(r == c, 1.0, 0.0).astype(jnp.float32)
-            factor_diag(s_ref)
-            w_ref[rows, rows] = jnp.where(c >= r, s_ref[:, :NB], 0.0)
-            li = s_ref[:, NB:]
-            inv_ref[pl.ds(pl.multiple_of(h * NB, NB), NB), pl.ds(pl.multiple_of(h * NB, NB), NB)] = li
-            loop(k + 1, N // NB, lambda j: w_ref.__setitem__((rows, ds(j, NB)), mm(li, w_ref[rows, ds(j, NB)])))
-
-            @pl.when(h == 0)
-            def _():
-                nxt = ds(k + 1, NB)
-                lhs = w_ref[rows, nxt]
-                def upd(j):
-                    w_ref[nxt, ds(j, NB)] = w_ref[nxt, ds(j, NB)] - mm_tn(lhs, w_ref[rows, ds(j, NB)])
-                loop(k + 1, N // NB, upd)
-
-        loop(0, 2, half)
-        pr = ds(p, PB)
-        i0 = inv_ref[:NB, :NB]
-        i1 = inv_ref[NB:, NB:]
-        u01 = w_ref[ds(2 * p, NB), ds(2 * p + 1, NB)]
-        inv_ref[NB:, :NB] = -mm(i1, mm_tn(u01, i0))
-        inv_ref[:NB, NB:] = jnp.zeros((NB, NB), jnp.float32)
-
-        def trail(i):
-            def cols(j):
-                w_ref[ds(i, PB), ds(j, PB)] = w_ref[ds(i, PB), ds(j, PB)] - mm_tn(w_ref[pr, ds(i, PB)], w_ref[pr, ds(j, PB)])
-            loop(i, NP, cols)
-        loop(p + 1, NP, trail)
-
-        def chunk(m):
-            rr = ds(m, PB)
-            def prev(t):
-                q_ref[rr, pr] = q_ref[rr, pr] - mm(q_ref[rr, ds(t, PB)], w_ref[ds(t, PB), pr])
-            loop(0, p, prev)
-            q_ref[rr, pr] = mm_nt(q_ref[rr, pr], inv_ref[...])
-        loop(0, N // PB, chunk)
-
-    loop(0, NP, panel)
-
-    def zero(k):
-        def zz(j):
-            w_ref[ds(k, NB), ds(j, NB)] = jnp.zeros((NB, NB), jnp.float32)
-        loop(0, k, zz)
-    loop(1, N // NB, zero)
-
-
-def fused_kernel(g_ref, b_ref, u_ref, q_ref, out_ref, s_ref, inv_ref, prev_ref, *rest):
-    unpack(g_ref, u_ref)
-    q_ref[...] = b_ref[...]
-    sweep_one(u_ref, q_ref, s_ref, inv_ref)
-    gram_reduce_kernel(q_ref, out_ref, *rest)
-
-
-def second_kernel(g_ref, b_ref, u1_ref, r_ref, q_ref, u_ref, s_ref, inv_ref, prev_ref):
-    unpack(g_ref, u_ref)
-    q_ref[...] = b_ref[...]
-    sweep_body(u_ref, q_ref, s_ref, inv_ref, prev_ref)
+    q_ref[...] = a_ref[...]
+    unpack(g_ref, w_ref.at[0])
+    for n in range(NP):
+        used = 64 * (n + 1)
+        if used < SIZES[n]:
+            sums[n].buf[used:] = jnp.zeros((SIZES[n] - used, TILE, NB), jnp.float32)
+
+    def gram_panel(n):
+        def block(t):
+            g = mm_tn(q_ref[:, ds(t, PB)], q_ref[:, n * PB:(n + 1) * PB])
+            for i in (0, 1):
+                for j in (0, 1):
+                    sums[n].buf[pl.ds((4 * t + 2 * i + j) * BT, BT)] = g[i * NB:(i + 1) * NB, j * NB:(j + 1) * NB].reshape(BT, TILE, NB)
+        loop(0, n + 1, block)
+
+    def unpack_panel(n):
+        def block(t):
+            for i in (0, 1):
+                for j in (0, 1):
+                    w_ref[1, ds(2 * t + i, NB), (2 * n + j) * NB:(2 * n + j + 1) * NB] = sums[n].out[pl.ds((4 * t + 2 * i + j) * BT, BT)].reshape(NB, NB)
+        loop(0, n + 1, block)
+
+    def service(point):
+        for stage, n in dict(POINTS)[point]:
+            if stage == 0:
+                gram_panel(n)
+                if n == 0:
+                    pl.semaphore_wait(barrier, len(peers))
+            sums[n].run(stage)
+            if stage == 7:
+                unpack_panel(n)
+
+    def update(m, s, d, rhs, keep):
+        rows = ds(m, PB)
+        base = jnp.where(keep, q_ref[rows, ds(d, PB)], 0.0)
+        q_ref[rows, ds(d, PB)] = base - mm(q_ref[rows, ds(s, PB)], rhs)
+
+    def solve(m, n):
+        q_ref[ds(m, PB), ds(n, PB)] = mm_nt(q_ref[ds(m, PB), ds(n, PB)], inv_ref[n])
+
+    def step(st):
+        sw = st // 8
+        k = lax.rem(st, 8)
+        p = k // 2
+        h = lax.rem(k, 2)
+        w = w_ref.at[sw]
+        q = jnp.maximum(p - 1, 0)
+        z = jnp.maximum(p - 2, 0)
+
+        @pl.when(h == 0)
+        def _():
+            def solved(t):
+                w[ds(t, PB), ds(p, PB)] = mm(inv_ref[t], w[ds(t, PB), ds(p, PB)])
+
+                def below(i):
+                    w[ds(i, PB), ds(p, PB)] = w[ds(i, PB), ds(p, PB)] - mm_tn(w[ds(t, PB), ds(i, PB)], w[ds(t, PB), ds(p, PB)])
+                loop(t + 1, p + 1, below)
+            loop(0, p, solved)
+            rhs_ref[0] = -inv_ref[q].T
+            rhs_ref[1] = w[ds(z, PB), ds(p, PB)]
+
+        @pl.when(h == 1)
+        def _():
+            rhs_ref[0] = w[ds(q, PB), ds(p, PB)]
+
+        @pl.when(p == 0)
+        def _():
+            rhs_ref[0] = jnp.zeros((PB, PB), jnp.float32)
+
+        @pl.when(p < 2)
+        def _():
+            rhs_ref[1] = jnp.zeros((PB, PB), jnp.float32)
+
+        keep = h + (p == 0).astype(jnp.int32) > 0
+        dst = jnp.where(h == 0, q, p)
+        tasks = [functools.partial(update, m, q, dst, rhs_ref[0], keep) for m in range(4)]
+        tasks += [functools.partial(update, 2 * h + m, z, p, rhs_ref[1], True) for m in range(2)]
+        rows = ds(k, NB)
+        s_ref[:, :NB] = w[rows, rows]
+        s_ref[:, NB:] = jnp.where(r == c, 1.0, 0.0).astype(jnp.float32)
+        factor_diag(s_ref, tasks)
+        w[rows, rows] = jnp.where(c >= r, s_ref[:, :NB], 0.0)
+        inv_ref[p, ds(h, NB), ds(h, NB)] = s_ref[:, NB:]
+
+        @pl.when(h == 0)
+        def _():
+            top, nxt = ds(k, NB), ds(k + 1, NB)
+            u01 = mm(inv_ref[p, :NB, :NB], w[top, nxt])
+            w[top, nxt] = u01
+            w[nxt, nxt] = w[nxt, nxt] - mm_tn(u01, u01)
+            w[nxt, top] = jnp.zeros((NB, NB), jnp.float32)
+
+        @pl.when(h == 1)
+        def _():
+            i0 = inv_ref[p, :NB, :NB]
+            i1 = inv_ref[p, NB:, NB:]
+            inv_ref[p, NB:, :NB] = -mm(i1, mm_tn(w[ds(k - 1, NB), ds(k, NB)], i0))
+            inv_ref[p, :NB, NB:] = jnp.zeros((NB, NB), jnp.float32)
+
+        @pl.when(k == 7)
+        def _():
+            loop(0, 4, lambda m: update(m, 0, 3, w[0:PB, 3 * PB:], True))
+
+        for point, _ in POINTS:
+            if point == int(point):
+                @pl.when(st == point)
+                def _(point=point):
+                    service(point)
+                    if point == 7:
+                        loop(0, 4, lambda m: solve(m, 3))
+                        service(7.3)
+                        service(7.6)
+
+    loop(0, 16, step)
+
+
+def finish_kernel(q_in, w_ref, inv_ref, r_ref, q_ref):
+    q_ref[...] = q_in[...]
+
+    def solve(m):
+        q_ref[ds(m, PB), 3 * PB:] = mm_nt(q_in[ds(m, PB), 3 * PB:], inv_ref[3])
+    loop(0, NP, solve)
     r_ref[...] = jnp.zeros((N, N), jnp.float32)
 
     def ri(i):
         def rj(j):
             def rk(k):
-                r_ref[ds(i, PB), ds(j, PB)] = r_ref[ds(i, PB), ds(j, PB)] + mm(u_ref[ds(i, PB), ds(k, PB)], u1_ref[ds(k, PB), ds(j, PB)])
+                r_ref[ds(i, PB), ds(j, PB)] = r_ref[ds(i, PB), ds(j, PB)] + mm(w_ref[1, ds(i, PB), ds(k, PB)], w_ref[0, ds(k, PB), ds(j, PB)])
             loop(i, j + 1, rk)
         loop(i, NP, rj)
     loop(0, NP, ri)
 
 
-SQ = jax.ShapeDtypeStruct((N, N), jnp.float32)
-WORK = [pltpu.VMEM((NB, 2 * NB), jnp.float32), pltpu.VMEM((PB, PB), jnp.float32), pltpu.VMEM((PB, PB), jnp.float32)]
-
-
-def first_sweep(g, a):
+def shape(*dims):
+    return jax.ShapeDtypeStruct(dims, jnp.float32)
+
+
+def sweeps(g, a):
+    f32 = jnp.float32
+    scratch = [pltpu.VMEM((NB, 2 * NB), f32), pltpu.VMEM((2, PB, PB), f32)]
+    for size in SIZES:
+        qa, qb = size // 24, size // 96
+        scratch += [pltpu.VMEM((size, TILE, NB), f32), pltpu.VMEM((size // 2, TILE, NB), f32), pltpu.VMEM((3, 3, qa, TILE, NB), f32), pltpu.VMEM((3, 3, qb, TILE, NB), f32), pltpu.VMEM((3, 4, qb, TILE, NB), f32), pltpu.VMEM((size, TILE, NB), f32)]
+        scratch += [pltpu.SemaphoreType.DMA((COPIES,)), pltpu.SemaphoreType.DMA((COPIES,))]
     return pl.pallas_call(
-        fused_kernel, out_shape=[SQ, SQ, jax.ShapeDtypeStruct((2 * HALF, TILE, NB), jnp.float32)], in_specs=[VM] * 2, out_specs=[VM] * 3, scratch_shapes=WORK + comm_scratch(),
+        sweeps_kernel, out_shape=[shape(N, N), shape(2, N, N), shape(NP, PB, PB)], in_specs=[VM] * 2, out_specs=[VM] * 3, scratch_shapes=scratch,
         compiler_params=pltpu.CompilerParams(vmem_limit_bytes=SWEEP_VMEM, collective_id=1, has_side_effects=True))(g, a)
 
 
-def second_sweep(g, q, u1):
-    return pl.pallas_call(second_kernel, out_shape=[SQ, SQ], in_specs=[VM] * 3, out_specs=[VM] * 2, scratch_shapes=[pltpu.VMEM((N, N), jnp.float32)] + WORK, compiler_params=pltpu.CompilerParams(vmem_limit_bytes=SWEEP_VMEM))(g, q, u1)
+def finish(q, w, inv):
+    return pl.pallas_call(finish_kernel, out_shape=[shape(N, N), shape(N, N)], in_specs=[VM] * 3, out_specs=[VM] * 2, compiler_params=pltpu.CompilerParams(vmem_limit_bytes=FINISH_VMEM))(q, w, inv)
 
 
 def solution(mesh):
     row_spec = P(("batch", "outer", "rows"), None)
 
     def group_qr(a_block):
-        u1, q1, g2 = first_sweep(gram_reduce(a_block, 0), a_block)
-        r_block, q_block = second_sweep(g2, q1, u1)
+        q, w, inv = sweeps(gram_reduce(a_block, 0), a_block)
+        r_block, q_block = finish(q, w, inv)
         return q_block, r_block
 
     return jax.shard_map(group_qr, mesh=mesh, in_specs=(row_spec,), out_specs=(row_spec, P("batch", None)), check_vma=False)

time: 208 us -> 185 us (0.89)
  Pallas kernels: 205 us -> 178 us
  local copies, waits for them, and re-layouts: 2.18 us -> 5.56 us
    pallas_call x2, Pallas kernels: 159 us -> 132 us  [the longest x1 119 us: sweeps(): pl.pallas_call(sweeps_kernel, out_shape=[shape(N, N), shape(2, N, N), sha...]
    unnamed x4 -> x6, local copies, waits for them, and re-layouts: 2.18 us -> 5.56 us
where the time goes in v2:
time: 185 us; the launch traced here: 184 us
  Pallas kernels  178 us (96%)
  local copies, waits for them, and re-layouts  5.56 us (3%)
    pallas_call x1, Pallas kernels, sweeps(): pl.pallas_call(sweeps_kernel, out_shape=[shape(N, N), shape(2, N, N), sha...  119 us
    pallas_call x1, Pallas kernels, gram_reduce(): pl.pallas_call(gram_reduce_kernel, out_shape=jax.ShapeDtypeStruct((2 * HA...  46.1 us
    pallas_call x1, Pallas kernels, finish(): pl.pallas_call(finish_kernel, out_shape=[shape(N, N), shape(N, N)], in_sp...  13.3 us
    unnamed x6, local copies, waits for them, and re-layouts  5.56 us

profile of v2, /device:TPU:1, one launch (start us, length us, event | category | flops | bytes accessed | tf_op | source)
XLA Modules:
  0.0 184.4 jit_solution(16452927829711823607)
XLA Ops:
  0.6 0.0 copy-start
  0.6 2.2 %copy-done = f32[1024,1024]{1,0:T(8,128)S(1)} copy-done((f32[1024,1024]{1,0:T(8,128)S(1)}, f32[1024,1024]{1,0:T(8,128)}, u32[]{:S(2)}) %copy-start) | copy-done | bytes 4194328
  2.8 0.0 copy-start.1
  2.8 46.1 %shard_map.30.g_ref = f32[576,8,128]{2,1,0:T(8,128)S(1)} custom-call(f32[1024,1024]{1,0:T(8,128)S(1)} %copy-done), custom_call_target="tpu_custom_call" | custom-call | tf_op jit(solution)/shard_map/pallas_call | solution.py:242
  48.9 0.0 copy-done.1
  49.0 118.8 %shard_map.31 = (f32[1024,1024]{1,0:T(8,128)S(1)}, f32[2,1024,1024]{2,1,0:T(8,128)}, f32[4,256,256]{2,1,0:T(8,128)S(1)}) custom-call(f32[576,8,128]{2,1,0:T(8,128)S(1)} %shard_map.30.g_ref, f32[1024,1024]{1,0:T(8,128)S(1)} %copy-done.1), custom_call_target="tpu_custom_call" | custom-call | tf_op jit(solution)/shard_map/pallas_call | solution.py:518
  167.8 0.0 copy-start.2
  167.8 3.4 %copy-done.2 = f32[2,1024,1024]{2,1,0:T(8,128)S(1)} copy-done((f32[2,1024,1024]{2,1,0:T(8,128)S(1)}, f32[2,1024,1024]{2,1,0:T(8,128)}, u32[]{:S(2)}) %copy-start.2) | copy-done | bytes 8388632
  171.2 13.3 %shard_map.32 = (f32[1024,1024]{1,0:T(8,128)}, f32[1024,1024]{1,0:T(8,128)}) custom-call(f32[1024,1024]{1,0:T(8,128)S(1)} %get-tuple-element.7.q_in, f32[2,1024,1024]{2,1,0:T(8,128)S(1)} %copy-done.2, f32[4,256,256]{2,1,0:T(8,128)S(1)} %get-tuple-element.9.inv_ref), custom_call_target="tpu_custom_call" | custom-call | tf_op jit(solution)/shard_map/pallas_call | solution.py:524
Async XLA Ops:
  0.6 2.2 %copy-start = (f32[1024,1024]{1,0:T(8,128)S(1)}, f32[1024,1024]{1,0:T(8,128)}, u32[]{:S(2)}) copy-start(f32[1024,1024]{1,0:T(8,128)} %a_ref.3) | copy-start | bytes 12582916
  2.8 46.1 %copy-start.1 = (f32[1024,1024]{1,0:T(8,128)S(1)}, f32[1024,1024]{1,0:T(8,128)}, u32[]{:S(2)}) copy-start(f32[1024,1024]{1,0:T(8,128)} %a_ref.3) | copy-start | bytes 12582916
  167.8 3.4 %copy-start.2 = (f32[2,1024,1024]{2,1,0:T(8,128)S(1)}, f32[2,1024,1024]{2,1,0:T(8,128)}, u32[]{:S(2)}) copy-start(f32[2,1024,1024]{2,1,0:T(8,128)} %get-tuple-element.8.w_ref) | copy-start | bytes 25165828

commit v3 on v2

v3 whole, which is shorter than its diff:
```python
import functools

import jax
import jax.numpy as jnp
from jax import lax
from jax.experimental import pallas as pl
from jax.experimental.pallas import tpu as pltpu
from jax.sharding import PartitionSpec as P

HI = lax.Precision.HIGHEST
N = 1024
NB = 128
SUB = 8


def mm(a, b):
    return lax.dot_general(a, b, (((1,), (0,)), ((), ())), precision=HI, preferred_element_type=jnp.float32)


def mm_tn(a, b):
    return lax.dot_general(a, b, (((0,), (0,)), ((), ())), precision=HI, preferred_element_type=jnp.float32)


def mm_nt(a, b):
    return lax.dot_general(a, b, (((1,), (1,)), ((), ())), precision=HI, preferred_element_type=jnp.float32)


def lane(v, c):
    return jnp.broadcast_to(v[:, c:c + 1], (SUB, NB))


PB = 256
NP = N // PB


def ds(i, n):
    return pl.ds(pl.multiple_of(i * n, n), n)


def loop(lo, hi, body):
    def step(i, carry):
        body(i)
        return carry
    lax.fori_loop(lo, hi, step, 0)


RG = 3


def factor_diag(s_ref, tasks=()):
    groups = NB // SUB
    tasks = list(tasks)
    for g in range(groups):
        base = SUB * g
        left = jnp.stack([jnp.broadcast_to(s_ref[base + i:base + i + 1, :NB], (SUB, NB)) for i in range(SUB)])
        right = jnp.stack([jnp.broadcast_to(s_ref[base + i:base + i + 1, NB:], (SUB, NB)) for i in range(SUB)])
        a = [jnp.stack([lane(left[j], base + i) for i in range(j, SUB)]) for j in range(SUB)]
        inv, u, rows = [], [], []
        for j in range(SUB):
            rs = lax.rsqrt(a[j][0])
            inv.append(rs)
            rl, rr = left[0] * rs, right[0] * rs
            rows.append((rl, rr))
            s_ref[base + j:base + j + 1, :NB] = rl[0:1]
            s_ref[base + j:base + j + 1, NB:] = rr[0:1]
            if j + 1 < SUB:
                uj = a[j][1:] * rs
                u.append(uj)
                for i in range(j + 1, SUB):
                    a[i] = a[i] - uj[i - j - 1:] * uj[i - j - 1]
                left = left[1:] - uj * rl
                right = right[1:] - uj * rr
        for lo in range(g + 1, groups, RG):
            hi = min(lo + RG, groups)
            n = hi - lo
            at = slice(SUB * lo, SUB * hi)
            bl = s_ref[at, :NB].reshape(n, SUB, NB)
            br = s_ref[at, NB:].reshape(n, SUB, NB)
            v = [jnp.broadcast_to(bl[:, :, base + j:base + j + 1], (n, SUB, NB)) for j in range(SUB)]
            for j in range(SUB):
                m = v[j] * inv[j]
                for j2 in range(j + 1, SUB):
                    v[j2] = v[j2] - m * u[j][j2 - j - 1]
                bl = bl - m * rows[j][0]
                br = br - m * rows[j][1]
            s_ref[at, :NB] = bl.reshape(n * SUB, NB)
            s_ref[at, NB:] = br.reshape(n * SUB, NB)
        if g % 2 == 1 and tasks:
            tasks.pop(0)()
    for task in tasks:
        task()


VM = pl.BlockSpec(memory_space=pltpu.VMEM)
SWEEP_VMEM = 30 * 1024 * 1024
FINISH_VMEM = 16 * 1024 * 1024
MESH = pl.DeviceIdType.MESH
TILE = 8
BT = NB // TILE
NBLK = N // NB
AXES = ((0, 1, 2), (1, 2, 0), (2, 0, 1))
STRIDE = (1, 4, 16)


SIZES = (96, 192, 192, 288)
COPIES = 1 + 9 * 5 + 12


class PanelSum:
    def __init__(self, n, buf, rcv0, rcva, rcvb, rcvc, out, s_snd, s_rcv, place):
        self.size = SIZES[n % NP]
        self.half = self.size // 2
        self.qa = self.half // 12
        self.qb = self.qa // 4
        self.buf, self.rcv0, self.rcva, self.rcvb, self.rcvc, self.out = buf, rcv0, rcva, rcvb, rcvc, out
        self.s_snd, self.s_rcv = s_snd, s_rcv
        self.core, self.pos, self.partner, self.near = place
        self.own = self.core * self.half
        self.other = self.half - self.own
        self.offsets = {}
        for c in range(3):
            self.offsets[c, 0] = self.own + c * (self.half // 3)
            self.offsets[c, 1] = self.offsets[c, 0] + self.qa * self.pos[AXES[c][0]]
            self.offsets[c, 2] = self.offsets[c, 1] + self.qb * self.pos[AXES[c][1]]

    def copy(self, k, src, dst, peer):
        return pltpu.make_async_remote_copy(src_ref=src, dst_ref=dst, send_sem=self.s_snd.at[k], recv_sem=self.s_rcv.at[k], device_id=peer, device_id_type=MESH)

    def offset(self, c, depth):
        return self.offsets[c, depth]

    def copies(self, stage):
        out = []
        for d in (1, 3, 2):
            for c in range(3):
                k = 1 + 9 * stage + 3 * (d - 1) + c
                axis = AXES[c][(0, 1, 2, 1, 0)[stage]]
                there, peer = self.near[axis, d]
                if stage == 0:
                    src, dst = self.buf.at[pl.ds(self.offset(c, 0) + self.qa * there, self.qa)], self.rcva.at[c, d - 1]
                elif stage == 1:
                    src, dst = self.buf.at[pl.ds(self.offset(c, 1) + self.qb * there, self.qb)], self.rcvb.at[c, d - 1]
                elif stage == 2:
                    src = dst = self.rcvc.at[c, self.pos[axis]]
                elif stage == 3:
                    src = dst = self.out.at[pl.ds(self.offset(c, 2), self.qb)]
                else:
                    src = dst = self.out.at[pl.ds(self.offset(c, 1), self.qa)]
                out.append(self.copy(k, src, dst, peer))
        return out

    def forwards(self):
        out = []
        for c in range(3):
            for d in range(4):
                axis = AXES[c][0]
                came = self.near[axis, 4 - d][0] if d else self.pos[axis]
                ref = self.out.at[pl.ds(self.offset(c, 0) + self.qa * came, self.qa)]
                out.append(self.copy(46 + 4 * c + d, ref, ref, self.partner))
        return out

    def swap(self):
        other = pl.ds(self.other, self.half)
        return self.copy(0, self.buf.at[other], self.rcv0, self.partner)

    def run(self, stage):
        if stage == 0:
            self.swap().start()
            return
        if stage == 1:
            self.swap().wait()
            at = pl.ds(self.own, self.half)
            self.buf[at] = self.buf[at] + self.rcv0[...]
        elif stage <= 6:
            for cp in self.copies(stage - 2):
                cp.wait()
        if stage == 2:
            for c in range(3):
                at = pl.ds(self.offset(c, 1), self.qa)
                self.buf[at] = (self.buf[at] + self.rcva[c, 0]) + (self.rcva[c, 1] + self.rcva[c, 2])
        elif stage == 3:
            for c in range(3):
                self.rcvc[c, self.pos[AXES[c][2]]] = (self.buf[pl.ds(self.offset(c, 2), self.qb)] + self.rcvb[c, 0]) + (self.rcvb[c, 1] + self.rcvb[c, 2])
        elif stage == 4:
            for c in range(3):
                self.out[pl.ds(self.offset(c, 2), self.qb)] = ((self.rcvc[c, 0] + self.rcvc[c, 1]) + self.rcvc[c, 2]) + self.rcvc[c, 3]
        if stage <= 5:
            for cp in self.copies(stage - 1):
                cp.start()
        elif stage == 6:
            for cp in self.forwards():
                cp.start()
        else:
            for cp in self.forwards():
                cp.wait()


START = (((0, 0),), ((0, 1), (1, 0)), ((0, 2), (2, 0), (1, 1)), ((0, 3), (3, 0), (2, 1), (1, 2)), ((4, 0), (3, 1), (2, 2), (1, 3)), ((5, 0), (4, 1), (3, 2), (2, 3)), ((6, 0), (5, 1), (4, 2), (3, 3)), ((7, 0),))
POINTS = {
    0: ((6, 1), (5, 2), (4, 3)), 1: ((7, 1), (6, 2), (5, 3)), 2: ((0, 4), (7, 2), (6, 3)), 3: ((1, 4), (7, 3)),
    4: ((2, 4), (0, 5)), 5: ((3, 4), (1, 5)), 6: ((4, 4), (2, 5), (0, 6)),
    7: ((5, 4), (3, 5), (1, 6)), 7.3: ((6, 4), (4, 5), (2, 6)), 7.6: ((0, 7), (7, 4), (5, 5), (3, 6)),
    8: ((1, 7), (6, 5), (4, 6)), 9: ((2, 7), (7, 5), (5, 6)), 10: ((3, 7), (6, 6)), 11: ((4, 7), (7, 6)),
    12: ((5, 7),), 13: ((6, 7), (7, 7))}


def sweeps_kernel(a_ref, q_ref, w_ref, inv_ref, s_ref, rhs_ref, *rest):
    core = lax.axis_index("outer")
    row = lax.axis_index("rows")
    pos = (lax.rem(row, 4), lax.rem(row // 4, 4), row // 16)
    partner = (0, 1 - core, row)

    def along(axis, d):
        there = lax.rem(pos[axis] + d, 4)
        return there, (0, core, row + (there - pos[axis]) * STRIDE[axis])

    barrier = pltpu.get_barrier_semaphore()
    near = {(axis, d): along(axis, d) for axis in range(3) for d in (1, 2, 3)}
    peers = [partner] + [peer for _, peer in near.values()]
    for peer in peers:
        pl.semaphore_signal(barrier, inc=1, device_id=peer, device_id_type=MESH)

    sums = [PanelSum(n, *rest[8 * n:8 * n + 8], (core, pos, partner, near)) for n in range(2 * NP)]
    r = lax.broadcasted_iota(jnp.int32, (NB, NB), 0)
    c = lax.broadcasted_iota(jnp.int32, (NB, NB), 1)
    for n in range(2 * NP):
        used = 64 * (n % NP + 1)
        if used < sums[n].size:
            sums[n].buf[used:] = jnp.zeros((sums[n].size - used, TILE, NB), jnp.float32)

    def gram_panel(n):
        ref, p = (a_ref, q_ref)[n // NP], n % NP

        def block(t):
            g = mm_tn(ref[:, ds(t, PB)], ref[:, p * PB:(p + 1) * PB])
            for i in (0, 1):
                for j in (0, 1):
                    sums[n].buf[pl.ds((4 * t + 2 * i + j) * BT, BT)] = g[i * NB:(i + 1) * NB, j * NB:(j + 1) * NB].reshape(BT, TILE, NB)
        loop(0, p + 1, block)

    def unpack_panel(n):
        sw, p = n // NP, n % NP

        def block(t):
            for i in (0, 1):
                for j in (0, 1):
                    w_ref[sw, ds(2 * t + i, NB), (2 * p + j) * NB:(2 * p + j + 1) * NB] = sums[n].out[pl.ds((4 * t + 2 * i + j) * BT, BT)].reshape(NB, NB)
        loop(0, p + 1, block)

    def service(stages):
        for stage, n in stages:
            if stage == 0:
                gram_panel(n)
                if n == 0:
                    pl.semaphore_wait(barrier, len(peers))
            sums[n].run(stage)
            if stage == 7:
                unpack_panel(n)

    def update(m, s, d, rhs, keep):
        rows = ds(m, PB)
        base = jnp.where(keep, q_ref[rows, ds(d, PB)], 0.0)
        q_ref[rows, ds(d, PB)] = base - mm(q_ref[rows, ds(s, PB)], rhs)

    def solve(m, n):
        q_ref[ds(m, PB), ds(n, PB)] = mm_nt(q_ref[ds(m, PB), ds(n, PB)], inv_ref[n])

    def step(st):
        sw = st // 8
        k = lax.rem(st, 8)
        p = k // 2
        h = lax.rem(k, 2)
        w = w_ref.at[sw]
        q = jnp.maximum(p - 1, 0)
        z = jnp.maximum(p - 2, 0)

        @pl.when(h == 0)
        def _():
            for n in range(1, NP):
                @pl.when(p == n)
                def _(n=n):
                    cols = slice(n * PB, (n + 1) * PB)
                    blocks = [w[t * PB:(t + 1) * PB, cols] for t in range(n + 1)]
                    for t in range(n):
                        top = slice(t * PB, (t + 1) * PB)
                        blocks[t] = mm(inv_ref[t], blocks[t])
                        w[top, cols] = blocks[t]
                        for i in range(t + 1, n):
                            blocks[i] = blocks[i] - mm_tn(w[top, i * PB:(i + 1) * PB], blocks[t])
                        blocks[n] = blocks[n] - mm_tn(blocks[t], blocks[t])
                    w[cols, cols] = blocks[n]
            rhs_ref[0] = -inv_ref[q].T
            rhs_ref[1] = w[ds(z, PB), ds(p, PB)]

        @pl.when(h == 1)
        def _():
            rhs_ref[0] = w[ds(q, PB), ds(p, PB)]

        @pl.when(p == 0)
        def _():
            rhs_ref[0] = jnp.zeros((PB, PB), jnp.float32)

        @pl.when(p < 2)
        def _():
            rhs_ref[1] = jnp.zeros((PB, PB), jnp.float32)

        keep = h + (p == 0).astype(jnp.int32) > 0
        dst = jnp.where(h == 0, q, p)
        tasks = [functools.partial(update, m, q, dst, rhs_ref[0], keep) for m in range(4)]
        tasks += [functools.partial(update, 2 * h + m, z, p, rhs_ref[1], True) for m in range(2)]
        rows = ds(k, NB)
        s_ref[:, :NB] = w[rows, rows]
        s_ref[:, NB:] = jnp.where(r == c, 1.0, 0.0).astype(jnp.float32)
        factor_diag(s_ref, tasks)
        w[rows, rows] = jnp.where(c >= r, s_ref[:, :NB], 0.0)
        inv_ref[p, ds(h, NB), ds(h, NB)] = s_ref[:, NB:]

        @pl.when(h == 0)
        def _():
            top, nxt = ds(k, NB), ds(k + 1, NB)
            i0 = inv_ref[p, :NB, :NB]
            u01 = mm(i0, w[top, nxt])
            inv_ref[p, NB:, :NB] = mm_tn(u01, i0)
            w[top, nxt] = u01
            w[nxt, nxt] = w[nxt, nxt] - mm_tn(u01, u01)
            w[nxt, top] = jnp.zeros((NB, NB), jnp.float32)

        @pl.when(h == 1)
        def _():
            inv_ref[p, NB:, :NB] = -mm(inv_ref[p, NB:, NB:], inv_ref[p, NB:, :NB])
            inv_ref[p, :NB, NB:] = jnp.zeros((NB, NB), jnp.float32)

        @pl.when(k == 7)
        def _():
            loop(0, 4, lambda m: update(m, 0, 3, w[0:PB, 3 * PB:], True))

        for point in POINTS:
            if point == int(point):
                @pl.when(st == point)
                def _(point=point):
                    service(POINTS[point])
                    if point == 7:
                        loop(0, 4, lambda m: solve(m, 3))
                        service(POINTS[7.3])
                        service(POINTS[7.6])

    for n, stages in enumerate(START):
        if n == 4:
            q_ref[...] = a_ref[...]
        service(stages)
    loop(0, 16, step)


def finish_kernel(q_in, w_ref, inv_ref, r_hbm, q_hbm, r_ref, q_ref, sems):
    ready = pltpu.make_async_copy(q_in.at[:, :3 * PB], q_hbm.at[:, :3 * PB], sems.at[0])
    ready.start()

    def solve(m):
        q_ref[ds(m, PB), :] = mm_nt(q_in[ds(m, PB), 3 * PB:], inv_ref[3])
    loop(0, NP, solve)
    rest = pltpu.make_async_copy(q_ref, q_hbm.at[:, 3 * PB:], sems.at[1])
    rest.start()
    r_ref[...] = jnp.zeros((N, N), jnp.float32)
    copies = [ready, rest]
    for i in range(NP):
        for j in range(i, NP):
            span = slice(i * PB, (j + 1) * PB)
            r_ref[i * PB:(i + 1) * PB, j * PB:(j + 1) * PB] = mm(w_ref[1, i * PB:(i + 1) * PB, span], w_ref[0, span, j * PB:(j + 1) * PB])
        copies.append(pltpu.make_async_copy(r_ref.at[i * PB:(i + 1) * PB], r_hbm.at[i * PB:(i + 1) * PB], sems.at[2 + i]))
        copies[-1].start()
    for cp in copies:
        cp.wait()


def shape(*dims):
    return jax.ShapeDtypeStruct(dims, jnp.float32)


def sweeps(a):
    f32 = jnp.float32
    scratch = [pltpu.VMEM((NB, 2 * NB), f32), pltpu.VMEM((2, PB, PB), f32)]
    for size in SIZES * 2:
        qa, qb = size // 24, size // 96
        scratch += [pltpu.VMEM((size, TILE, NB), f32), pltpu.VMEM((size // 2, TILE, NB), f32), pltpu.VMEM((3, 3, qa, TILE, NB), f32), pltpu.VMEM((3, 3, qb, TILE, NB), f32), pltpu.VMEM((3, 4, qb, TILE, NB), f32), pltpu.VMEM((size, TILE, NB), f32)]
        scratch += [pltpu.SemaphoreType.DMA((COPIES,)), pltpu.SemaphoreType.DMA((COPIES,))]
    return pl.pallas_call(
        sweeps_kernel, out_shape=[shape(N, N), shape(2, N, N), shape(NP, PB, PB)], in_specs=[VM], out_specs=[VM] * 3, scratch_shapes=scratch,
        compiler_params=pltpu.CompilerParams(vmem_limit_bytes=SWEEP_VMEM, collective_id=0, has_side_effects=True))(a)


def finish(q, w, inv):
    return pl.pallas_call(finish_kernel, out_shape=[shape(N, N), shape(N, N)], in_specs=[VM] * 3, out_specs=[pl.BlockSpec(memory_space=pl.ANY)] * 2, scratch_shapes=[pltpu.VMEM((N, N), jnp.float32), pltpu.VMEM((N, PB), jnp.float32), pltpu.SemaphoreType.DMA((2 + NP,))], compiler_params=pltpu.CompilerParams(vmem_limit_bytes=FINISH_VMEM))(q, w, inv)


def solution(mesh):
    row_spec = P(("batch", "outer", "rows"), None)

    def group_qr(a_block):
        q, w, inv = sweeps(a_block)
        r_block, q_block = finish(q, w, inv)
        return q_block, r_block

    return jax.shard_map(group_qr, mesh=mesh, in_specs=(row_spec,), out_specs=(row_spec, P("batch", None)), check_vma=False)
```

time: 185 us -> 160 us (0.86)
  Pallas kernels: 178 us -> 157 us
  local copies, waits for them, and re-layouts: 5.56 us -> 2.18 us
    pallas_call x1 -> x0, Pallas kernels: 46.1 us -> none  [gram_reduce(): pl.pallas_call(gram_reduce_kernel, out_shape=jax.ShapeDtypeStruct((2 * HA...]
    pallas_call x1, Pallas kernels: 119 us -> 149 us  [sweeps(): pl.pallas_call(sweeps_kernel, out_shape=[shape(N, N), shape(2, N, N), sha...]
    pallas_call x1, Pallas kernels: 13.3 us -> 8.11 us  [finish(): pl.pallas_call(finish_kernel, out_shape=[shape(N, N), shape(N, N)], in_sp...]
    unnamed x6 -> x2, local copies, waits for them, and re-layouts: 5.56 us -> 2.18 us
where the time goes in v3:
time: 160 us
  Pallas kernels  157 us (98%)
  local copies, waits for them, and re-layouts  2.18 us (1%)
    pallas_call x1, Pallas kernels, sweeps(): pl.pallas_call(sweeps_kernel, out_shape=[shape(N, N), shape(2, N, N), sha...  149 us
    pallas_call x1, Pallas kernels, finish(): pl.pallas_call(finish_kernel, out_shape=[shape(N, N), shape(N, N)], in_sp...  8.11 us

profile of v3, /device:TPU:1, one launch (start us, length us, event | category | flops | bytes accessed | tf_op | source)
XLA Modules:
  0.0 159.7 jit_solution(12416436258910381424)
XLA Ops:
  0.6 0.0 copy-start
  0.6 2.2 %copy-done = f32[1024,1024]{1,0:T(8,128)S(1)} copy-done((f32[1024,1024]{1,0:T(8,128)S(1)}, f32[1024,1024]{1,0:T(8,128)}, u32[]{:S(2)}) %copy-start) | copy-done | bytes 4194328
  2.8 148.6 %shard_map.30 = (f32[1024,1024]{1,0:T(8,128)S(1)}, f32[2,1024,1024]{2,1,0:T(8,128)S(1)}, f32[4,256,256]{2,1,0:T(8,128)S(1)}) custom-call(f32[1024,1024]{1,0:T(8,128)S(1)} %copy-done), custom_call_target="tpu_custom_call" | custom-call | tf_op jit(solution)/shard_map/pallas_call | solution.py:386
  151.4 8.1 %shard_map.31 = (f32[1024,1024]{1,0:T(8,128)}, f32[1024,1024]{1,0:T(8,128)}) custom-call(f32[1024,1024]{1,0:T(8,128)S(1)} %get-tuple-element.7.q_in, f32[2,1024,1024]{2,1,0:T(8,128)S(1)} %get-tuple-element.8.w_ref, f32[4,256,256]{2,1,0:T(8,128)S(1)} %get-tuple-element.9.inv_ref), custom_call_target="tpu_custom_call" | custom-call | tf_op jit(solution)/shard_map/pallas_call | solution.py:392
Async XLA Ops:
  0.6 2.2 %copy-start = (f32[1024,1024]{1,0:T(8,128)S(1)}, f32[1024,1024]{1,0:T(8,128)}, u32[]{:S(2)}) copy-start(f32[1024,1024]{1,0:T(8,128)} %a_ref.1) | copy-start | bytes 12582916

commit v4 on v3

--- a/solution.py
+++ b/solution.py
@@ -112,6 +112,7 @@
         self.half = self.size // 2
         self.qa = self.half // 12
         self.qb = self.qa // 4
+        self.flat = n % NP == 0
         self.buf, self.rcv0, self.rcva, self.rcvb, self.rcvc, self.out = buf, rcv0, rcva, rcvb, rcvc, out
         self.s_snd, self.s_rcv = s_snd, s_rcv
         self.core, self.pos, self.partner, self.near = place
@@ -138,6 +139,8 @@
                 there, peer = self.near[axis, d]
                 if stage == 0:
                     src, dst = self.buf.at[pl.ds(self.offset(c, 0) + self.qa * there, self.qa)], self.rcva.at[c, d - 1]
+                elif stage == 1 and self.flat:
+                    src = dst = self.rcvb.at[c, self.pos[axis]]
                 elif stage == 1:
                     src, dst = self.buf.at[pl.ds(self.offset(c, 1) + self.qb * there, self.qb)], self.rcvb.at[c, d - 1]
                 elif stage == 2:
@@ -162,6 +165,9 @@
     def swap(self):
         other = pl.ds(self.other, self.half)
         return self.copy(0, self.buf.at[other], self.rcv0, self.partner)
+
+    def in_order(self, ref, c):
+        return ((ref[c, 0] + ref[c, 1]) + ref[c, 2]) + ref[c, 3]
 
     def run(self, stage):
         if stage == 0:
@@ -177,15 +183,23 @@
         if stage == 2:
             for c in range(3):
                 at = pl.ds(self.offset(c, 1), self.qa)
-                self.buf[at] = (self.buf[at] + self.rcva[c, 0]) + (self.rcva[c, 1] + self.rcva[c, 2])
+                total = (self.buf[at] + self.rcva[c, 0]) + (self.rcva[c, 1] + self.rcva[c, 2])
+                if self.flat:
+                    self.rcvb[c, self.pos[AXES[c][1]]] = total
+                else:
+                    self.buf[at] = total
+        elif stage == 3 and self.flat:
+            for c in range(3):
+                self.rcvc[c, self.pos[AXES[c][2]]] = self.in_order(self.rcvb, c)
         elif stage == 3:
             for c in range(3):
                 self.rcvc[c, self.pos[AXES[c][2]]] = (self.buf[pl.ds(self.offset(c, 2), self.qb)] + self.rcvb[c, 0]) + (self.rcvb[c, 1] + self.rcvb[c, 2])
         elif stage == 4:
             for c in range(3):
-                self.out[pl.ds(self.offset(c, 2), self.qb)] = ((self.rcvc[c, 0] + self.rcvc[c, 1]) + self.rcvc[c, 2]) + self.rcvc[c, 3]
+                at = pl.ds(self.offset(c, 1), self.qa) if self.flat else pl.ds(self.offset(c, 2), self.qb)
+                self.out[at] = self.in_order(self.rcvc, c)
         if stage <= 5:
-            for cp in self.copies(stage - 1):
+            for cp in self.copies(4 if self.flat and stage == 4 else stage - 1):
                 cp.start()
         elif stage == 6:
             for cp in self.forwards():
@@ -195,16 +209,19 @@
                 cp.wait()
 
 
-START = (((0, 0),), ((0, 1), (1, 0)), ((0, 2), (2, 0), (1, 1)), ((0, 3), (3, 0), (2, 1), (1, 2)), ((4, 0), (3, 1), (2, 2), (1, 3)), ((5, 0), (4, 1), (3, 2), (2, 3)), ((6, 0), (5, 1), (4, 2), (3, 3)), ((7, 0),))
+START = (
+    ((0, 0, 1), ((0, 0),)), ((1, 0, 2), ((1, 0), (0, 1))), ((2, 0, 3), ((2, 0), (0, 2), (1, 1))),
+    ((3, 0, 2), ((3, 0), (2, 1), (1, 2))), ((3, 2, 4), ((0, 3), (4, 0), (3, 1), (2, 2))),
+    (None, ((6, 0), (4, 1), (3, 2), (1, 3))), (None, ((7, 0), (5, 1))))
 POINTS = {
-    0: ((6, 1), (5, 2), (4, 3)), 1: ((7, 1), (6, 2), (5, 3)), 2: ((0, 4), (7, 2), (6, 3)), 3: ((1, 4), (7, 3)),
-    4: ((2, 4), (0, 5)), 5: ((3, 4), (1, 5)), 6: ((4, 4), (2, 5), (0, 6)),
-    7: ((5, 4), (3, 5), (1, 6)), 7.3: ((6, 4), (4, 5), (2, 6)), 7.6: ((0, 7), (7, 4), (5, 5), (3, 6)),
+    0: ((6, 1), (4, 2), (2, 3)), 1: ((7, 1), (5, 2), (3, 3)), 2: ((0, 4), (6, 2), (4, 3)), 3: ((1, 4), (7, 2), (5, 3)),
+    4: ((2, 4), (0, 5), (6, 3)), 5: ((3, 4), (1, 5), (7, 3)), 6: ((4, 4), (2, 5), (0, 6)),
+    7: ((6, 4), (3, 5), (1, 6)), 7.3: ((7, 4), (4, 5), (2, 6)), 7.6: ((0, 7), (5, 5), (3, 6)),
     8: ((1, 7), (6, 5), (4, 6)), 9: ((2, 7), (7, 5), (5, 6)), 10: ((3, 7), (6, 6)), 11: ((4, 7), (7, 6)),
     12: ((5, 7),), 13: ((6, 7), (7, 7))}
 
 
-def sweeps_kernel(a_ref, q_ref, w_ref, inv_ref, s_ref, rhs_ref, *rest):
+def sweeps_kernel(a_ref, q_ref, w_ref, inv_ref, s_ref, rhs_ref, s_in, *rest):
     core = lax.axis_index("outer")
     row = lax.axis_index("rows")
     pos = (lax.rem(row, 4), lax.rem(row // 4, 4), row // 16)
@@ -213,6 +230,10 @@
     def along(axis, d):
         there = lax.rem(pos[axis] + d, 4)
         return there, (0, core, row + (there - pos[axis]) * STRIDE[axis])
+
+    fetch = [pltpu.make_async_copy(a_ref.at[:, n * PB:(n + 1) * PB], q_ref.at[:, n * PB:(n + 1) * PB], s_in.at[n]) for n in range(NP)]
+    for cp in fetch:
+        cp.start()
 
     barrier = pltpu.get_barrier_semaphore()
     near = {(axis, d): along(axis, d) for axis in range(3) for d in (1, 2, 3)}
@@ -228,15 +249,15 @@
         if used < sums[n].size:
             sums[n].buf[used:] = jnp.zeros((sums[n].size - used, TILE, NB), jnp.float32)
 
-    def gram_panel(n):
-        ref, p = (a_ref, q_ref)[n // NP], n % NP
+    def gram_panel(n, lo, hi):
+        p = n % NP
 
         def block(t):
-            g = mm_tn(ref[:, ds(t, PB)], ref[:, p * PB:(p + 1) * PB])
+            g = mm_tn(q_ref[:, ds(t, PB)], q_ref[:, p * PB:(p + 1) * PB])
             for i in (0, 1):
                 for j in (0, 1):
                     sums[n].buf[pl.ds((4 * t + 2 * i + j) * BT, BT)] = g[i * NB:(i + 1) * NB, j * NB:(j + 1) * NB].reshape(BT, TILE, NB)
-        loop(0, p + 1, block)
+        loop(lo, hi, block)
 
     def unpack_panel(n):
         sw, p = n // NP, n % NP
@@ -249,10 +270,8 @@
 
     def service(stages):
         for stage, n in stages:
-            if stage == 0:
-                gram_panel(n)
-                if n == 0:
-                    pl.semaphore_wait(barrier, len(peers))
+            if stage == 0 and n >= NP:
+                gram_panel(n, 0, n - NP + 1)
             sums[n].run(stage)
             if stage == 7:
                 unpack_panel(n)
@@ -289,20 +308,15 @@
                             blocks[i] = blocks[i] - mm_tn(w[top, i * PB:(i + 1) * PB], blocks[t])
                         blocks[n] = blocks[n] - mm_tn(blocks[t], blocks[t])
                     w[cols, cols] = blocks[n]
-            rhs_ref[0] = -inv_ref[q].T
-            rhs_ref[1] = w[ds(z, PB), ds(p, PB)]
-
-        @pl.when(h == 1)
+                    rhs_ref[0] = -inv_ref[n - 1].T
+                    rhs_ref[1] = blocks[n - 2] if n > 1 else jnp.zeros((PB, PB), jnp.float32)
+            @pl.when(p == 0)
+            def _():
+                rhs_ref[...] = jnp.zeros((2, PB, PB), jnp.float32)
+
+        @pl.when(h * p > 0)
         def _():
             rhs_ref[0] = w[ds(q, PB), ds(p, PB)]
-
-        @pl.when(p == 0)
-        def _():
-            rhs_ref[0] = jnp.zeros((PB, PB), jnp.float32)
-
-        @pl.when(p < 2)
-        def _():
-            rhs_ref[1] = jnp.zeros((PB, PB), jnp.float32)
 
         keep = h + (p == 0).astype(jnp.int32) > 0
         dst = jnp.where(h == 0, q, p)
@@ -332,7 +346,7 @@
 
         @pl.when(k == 7)
         def _():
-            loop(0, 4, lambda m: update(m, 0, 3, w[0:PB, 3 * PB:], True))
+            loop(0, 2, lambda m: (update(2 * m, 0, 3, w[0:PB, 3 * PB:], True), update(2 * m + 1, 0, 3, w[0:PB, 3 * PB:], True)))
 
         for point in POINTS:
             if point == int(point):
@@ -340,13 +354,17 @@
                 def _(point=point):
                     service(POINTS[point])
                     if point == 7:
-                        loop(0, 4, lambda m: solve(m, 3))
+                        loop(0, 2, lambda m: (solve(2 * m, 3), solve(2 * m + 1, 3)))
                         service(POINTS[7.3])
                         service(POINTS[7.6])
 
-    for n, stages in enumerate(START):
-        if n == 4:
-            q_ref[...] = a_ref[...]
+    for gram, stages in START:
+        if gram:
+            if gram[1] == 0:
+                fetch[gram[0]].wait()
+            gram_panel(*gram)
+        if gram == (0, 0, 1):
+            pl.semaphore_wait(barrier, len(peers))
         service(stages)
     loop(0, 16, step)
 
@@ -357,7 +375,7 @@
 
     def solve(m):
         q_ref[ds(m, PB), :] = mm_nt(q_in[ds(m, PB), 3 * PB:], inv_ref[3])
-    loop(0, NP, solve)
+    loop(0, 2, lambda m: (solve(2 * m), solve(2 * m + 1)))
     rest = pltpu.make_async_copy(q_ref, q_hbm.at[:, 3 * PB:], sems.at[1])
     rest.start()
     r_ref[...] = jnp.zeros((N, N), jnp.float32)
@@ -378,13 +396,14 @@
 
 def sweeps(a):
     f32 = jnp.float32
-    scratch = [pltpu.VMEM((NB, 2 * NB), f32), pltpu.VMEM((2, PB, PB), f32)]
-    for size in SIZES * 2:
+    scratch = [pltpu.VMEM((NB, 2 * NB), f32), pltpu.VMEM((2, PB, PB), f32), pltpu.SemaphoreType.DMA((NP,))]
+    for n, size in enumerate(SIZES * 2):
         qa, qb = size // 24, size // 96
-        scratch += [pltpu.VMEM((size, TILE, NB), f32), pltpu.VMEM((size // 2, TILE, NB), f32), pltpu.VMEM((3, 3, qa, TILE, NB), f32), pltpu.VMEM((3, 3, qb, TILE, NB), f32), pltpu.VMEM((3, 4, qb, TILE, NB), f32), pltpu.VMEM((size, TILE, NB), f32)]
+        late = qa if n % NP == 0 else qb
+        scratch += [pltpu.VMEM((size, TILE, NB), f32), pltpu.VMEM((size // 2, TILE, NB), f32), pltpu.VMEM((3, 3, qa, TILE, NB), f32), pltpu.VMEM((3, 4, late, TILE, NB), f32), pltpu.VMEM((3, 4, late, TILE, NB), f32), pltpu.VMEM((size, TILE, NB), f32)]
         scratch += [pltpu.SemaphoreType.DMA((COPIES,)), pltpu.SemaphoreType.DMA((COPIES,))]
     return pl.pallas_call(
-        sweeps_kernel, out_shape=[shape(N, N), shape(2, N, N), shape(NP, PB, PB)], in_specs=[VM], out_specs=[VM] * 3, scratch_shapes=scratch,
+        sweeps_kernel, out_shape=[shape(N, N), shape(2, N, N), shape(NP, PB, PB)], in_specs=[pl.BlockSpec(memory_space=pltpu.HBM)], out_specs=[VM] * 3, scratch_shapes=scratch,
         compiler_params=pltpu.CompilerParams(vmem_limit_bytes=SWEEP_VMEM, collective_id=0, has_side_effects=True))(a)
 
 

time: 160 us -> 157 us (0.981)
  Pallas kernels: 157 us -> 154 us
    pallas_call x1, Pallas kernels: 149 us -> 146 us  [sweeps(): pl.pallas_call(sweeps_kernel, out_shape=[shape(N, N), shape(2, N, N), sha...]
where the time goes in v4:
time: 157 us
  Pallas kernels  154 us (98%)
  local copies, waits for them, and re-layouts  2.18 us (1%)
    pallas_call x1, Pallas kernels, sweeps(): pl.pallas_call(sweeps_kernel, out_shape=[shape(N, N), shape(2, N, N), sha...  146 us
    pallas_call x1, Pallas kernels, finish(): pl.pallas_call(finish_kernel, out_shape=[shape(N, N), shape(N, N)], in_sp...  7.69 us

profile of v4, /device:TPU:1, one launch (start us, length us, event | category | flops | bytes accessed | tf_op | source)
XLA Modules:
  0.0 157.2 jit_solution(522612970184236731)
XLA Ops:
  0.6 0.0 copy-start
  0.6 2.2 %copy-done = f32[1024,1024]{1,0:T(8,128)S(1)} copy-done((f32[1024,1024]{1,0:T(8,128)S(1)}, f32[1024,1024]{1,0:T(8,128)}, u32[]{:S(2)}) %copy-start) | copy-done | bytes 4194328
  2.8 146.5 %shard_map.30 = (f32[1024,1024]{1,0:T(8,128)S(1)}, f32[2,1024,1024]{2,1,0:T(8,128)S(1)}, f32[4,256,256]{2,1,0:T(8,128)S(1)}) custom-call(f32[1024,1024]{1,0:T(8,128)S(1)} %copy-done), custom_call_target="tpu_custom_call" | custom-call | tf_op jit(solution)/shard_map/pallas_call | solution.py:405
  149.3 7.7 %shard_map.31 = (f32[1024,1024]{1,0:T(8,128)}, f32[1024,1024]{1,0:T(8,128)}) custom-call(f32[1024,1024]{1,0:T(8,128)S(1)} %get-tuple-element.7.q_in, f32[2,1024,1024]{2,1,0:T(8,128)S(1)} %get-tuple-element.8.w_ref, f32[4,256,256]{2,1,0:T(8,128)S(1)} %get-tuple-element.9.inv_ref), custom_call_target="tpu_custom_call" | custom-call | tf_op jit(solution)/shard_map/pallas_call | solution.py:411
Async XLA Ops:
  0.6 2.2 %copy-start = (f32[1024,1024]{1,0:T(8,128)S(1)}, f32[1024,1024]{1,0:T(8,128)}, u32[]{:S(2)}) copy-start(f32[1024,1024]{1,0:T(8,128)} %a_ref.1) | copy-start | bytes 12582916
